TPU v7x, 32 devices: a 4x2x2 block of a 4x4x8 slice. The times are simulated.
32 devices in a mesh: dp: 4 (over y, z), tp: 8 (over x, core).
Axes of the slice: x: 4, y: 2, z: 2, core: 2. Of those that a mesh axis runs over, the one named last changes fastest.
The devices are a block of a 4x4x8 slice.
Arguments:
- hidden: bfloat16 [512, 4096], P('dp'), parts along dimension 0
- w_gate: bfloat16 [4096, 14336], P(None, 'tp')
- w_up: bfloat16 [4096, 14336], P(None, 'tp')
- w_down: bfloat16 [14336, 4096], P('tp')
- norm_gain: float32 [4096], replicated
- w_vocab: bfloat16 [4096, 32768], P(None, 'tp')
- temperature: float32 [512], P('dp'), parts along dimension 0
- target: int32 [512], P('dp'), parts along dimension 0
Outputs:
- output 1: float32 [512], P('dp'), parts along dimension 0
- output 2: float32 [512], P('dp'), parts along dimension 0
- output 3: float32 [512], P('dp'), parts along dimension 0
- output 4: bfloat16 [512, 32768], P('dp'), parts along dimension 0
There are 4 independent parts. A program takes and returns all parts, laid end to end along the dimension named above; an argument that names none is the same for every part.
All inputs are finite; a program needn't handle non-finite values.
Results may differ from a plain program's by a relative error of at most 0.00436137.
Values are sent between devices in bfloat16 or wider.
A program may use at most 768 MiB of HBM per device.

v0:
```python
import jax
import jax.numpy as jnp
from jax import lax
from jax.sharding import PartitionSpec as P

NORM_EPS = 1e-6


def solution(mesh):
    def device_step(hidden, w_gate, w_up, w_down, norm_gain, w_vocab, value_a11, target):
        gate_pre = jnp.dot(hidden, w_gate, preferred_element_type=jnp.float32)
        up_pre = jnp.dot(hidden, w_up, preferred_element_type=jnp.float32)
        hidden_act = (jax.nn.silu(gate_pre) * up_pre).astype(jnp.bfloat16)
        part_sum = jnp.dot(hidden_act, w_down, preferred_element_type=jnp.float32).astype(jnp.bfloat16)
        mlp_out = lax.psum(part_sum, "tp")
        residual = hidden.astype(jnp.float32) + mlp_out.astype(jnp.float32)
        inv_rms = lax.rsqrt(jnp.mean(residual * residual, axis=-1, keepdims=True) + NORM_EPS)
        normed = (norm_gain * residual * inv_rms).astype(jnp.bfloat16)
        logits = jnp.dot(normed, w_vocab, preferred_element_type=jnp.float32) / value_a11[:, None]
        vocab_local = logits.shape[1]
        row_max = lax.pmax(jnp.max(logits, axis=-1), "tp")
        shifted = jnp.exp(logits - row_max[:, None])
        local_ids = target - lax.axis_index("tp") * vocab_local
        col_ids = jnp.arange(vocab_local, dtype=jnp.int32)
        target_hit = jnp.where(col_ids[None, :] == local_ids[:, None], logits, 0.0)
        local_stats = jnp.stack(
            [jnp.sum(shifted, axis=-1), jnp.sum(shifted * logits, axis=-1), jnp.sum(target_hit, axis=-1)], axis=0)
        row_stats = lax.psum(local_stats, "tp")
        sum_exp = row_stats[0]
        weighted_sum = row_stats[1]
        target_logit = row_stats[2]
        log_norm = row_max + jnp.log(sum_exp)
        entropy = log_norm - weighted_sum / sum_exp
        target_logp = target_logit - log_norm
        local_probs = (logits - log_norm[:, None]).astype(jnp.bfloat16)
        log_probs = lax.all_gather(local_probs, "tp", axis=1, tiled=True)
        return log_norm, entropy, target_logp, log_probs

    return jax.shard_map(
        device_step,
        mesh=mesh,
        in_specs=(P("dp", None), P(None, "tp"), P(None, "tp"), P("tp", None), P(None),
                  P(None, "tp"), P("dp"), P("dp")),
        out_specs=(P("dp"), P("dp"), P("dp"), P("dp", None)),
        check_vma=False,
    )
```

profile of v0, /device:TPU:81, one launch (start us, length us, event | category | flops | bytes accessed | tf_op | source)
XLA Modules:
  0.0 194.0 jit_solution(16281841588875522326)
XLA Ops:
  7.2 0.0 copy-start
  7.2 0.1 all-reduce.2.cloned.1.call-start
  7.3 7.6 %fusion.7 = f32[128,1792]{1,0:T(8,128)S(1)} fusion(bf16[128,4096]{1,0:T(8,128)(2,1)} %param.8, bf16[4096,1792]{1,0:T(8,128)(2,1)} %param.9), kind=kOutput, calls=%fused_computation.25 | convolution fusion | flops 1879048192 | bytes 16646144 | tf_op jit(solution)/shard_map/dot_general | solution.py:11
  14.9 0.0 copy-done
  14.9 0.0 copy-start.4
  14.9 14.7 %convolution_convert_fusion = bf16[128,4096]{1,0:T(8,128)(2,1)} fusion(bf16[1792,4096]{1,0:T(8,128)(2,1)} %param.11, bf16[128,4096]{1,0:T(8,128)(2,1)S(1)} %copy-done, bf16[4096,1792]{1,0:T(8,128)(2,1)} %param.10, f32[128,1792]{1,0:T(8,128)S(1)} %fusion.7), kind=kOutput, calls=%fused_computation | convolution fusion | flops 3759996928 | bytes 32374784 | tf_op jit(solution)/shard_map/dot_general | solution.py:14
  29.7 0.0 copy-start.3
  29.7 0.0 copy-start.5
  29.7 0.1 all-reduce.2.cloned.1.call-update
  29.7 0.1 all-gather.2.cloned.1.call-start
  29.8 0.0 copy-done.4
  29.8 58.4 %all-reduce.2.cloned.1.call-done = bf16[128,4096]{1,0:T(8,128)(2,1)} async-done(((bf16[128,4096]{1,0:T(8,128)(2,1)}), bf16[128,4096]{1,0:T(8,128)(2,1)}) %all-reduce.2.cloned.1.call-update) | async-done | bytes 1048592 | tf_op jit(solution)/shard_map/psum | solution.py:15
  88.2 0.0 copy-start.1
  88.2 1.7 multiply_reduce_fusion.1
  90.0 0.0 copy-done.3
  90.0 0.0 copy-done.5
  90.0 0.0 copy-done.1
  90.0 13.3 %fusion.6 = (f32[128]{0:T(128)S(1)}, f32[128,4096]{1,0:T(8,128)S(1)}) fusion(f32[128]{0:T(128)S(1)} %copy-done.5, bf16[4096,4096]{1,0:T(8,128)(2,1)} %param.13, bf16[128,4096]{1,0:T(8,128)(2,1)S(1)} %copy-done.1, bf16[128,4096]{1,0:T(8,128)(2,1)S(1)} %copy-done, f32[128]{0:T(128)S(1)} %add_rsqrt_fusion, f32[4096]{0:T(1024)S(1)} %copy-done.3), kind=kOutput, calls=%fused_computation.24 | convolution fusion | flops 4299161600 | bytes 37766656 | tf_op jit(solution)/shard_map/dot_general | solution.py:19
  103.3 14.6 %pmax.7 = f32[128]{0:T(128)S(1)} all-reduce(f32[128]{0:T(128)S(1)} %get-tuple-element.9), channel_id=1, replica_groups=mesh['dp'=4,'tp'=8] {'tp'}, use_global_device_ids=true, to_apply=%region_3.4 | all-reduce | flops 128 | bytes 1024 | tf_op jit(solution)/shard_map/pmax | solution.py:21
  118.0 0.8 fusion.1
  118.8 13.4 %psum.15 = f32[3,128]{1,0:T(4,128)S(1)} all-reduce(f32[3,128]{1,0:T(4,128)S(1)} %pad_maximum_fusion), channel_id=1, replica_groups=mesh['dp'=4,'tp'=8] {'tp'}, use_global_device_ids=true, to_apply=%region_7.8 | all-reduce | flops 384 | bytes 3072 | tf_op jit(solution)/shard_map/psum | solution.py:28
  132.1 0.5 bitcast_subtract_fusion
  132.6 0.0 copy-start.2
  132.6 1.2 subtract_convert_fusion
  133.8 0.1 all-gather.2.cloned.1.call-update
  133.9 0.0 copy-done.2
  133.9 0.5 bitcast_subtract_fusion.1
  134.4 45.2 %all-gather.2.cloned.1.call-done = bf16[128,32768]{1,0:T(8,128)(2,1)} async-done(((bf16[128,4096]{1,0:T(8,128)(2,1)}), bf16[128,32768]{1,0:T(8,128)(2,1)}) %all-gather.2.cloned.1.call-update) | async-done | bytes 8388624 | tf_op jit(solution)/shard_map/all_gather | solution.py:36
  179.6 7.5 %copy.14 = bf16[128,32768]{1,0:T(8,128)(2,1)} copy(bf16[128,32768]{1,0:T(8,128)(2,1)} %all-gather.2.cloned.1.call-done) | data formatting | bytes 16777216
  (3 shorter events, 0.0 us)
Async XLA Ops:
  7.2 7.7 %copy-start = (bf16[128,4096]{1,0:T(8,128)(2,1)S(1)}, bf16[128,4096]{1,0:T(8,128)(2,1)}, u32[]{:S(2)}) copy-start(bf16[128,4096]{1,0:T(8,128)(2,1)} %param.8) | copy-start | bytes 3145732
  7.2 81.0 %all-reduce.2.cloned.1.call-start = ((), (), s32[]{:S(2)}) async-start(), calls=%async_computation | async-start | bytes 2097152 | tf_op jit(solution)/shard_map/psum | solution.py:15
  14.9 14.9 %copy-start.4 = (s32[128]{0:T(128)S(1)}, s32[128]{0:T(128)}, u32[]{:S(2)}) copy-start(s32[128]{0:T(128)} %param.15) | copy-start | bytes 1540
  29.7 60.3 %copy-start.3 = (f32[4096]{0:T(1024)S(1)}, f32[4096]{0:T(1024)}, u32[]{:S(2)}) copy-start(f32[4096]{0:T(1024)} %param.12) | copy-start | bytes 49156
  29.7 60.3 %copy-start.5 = (f32[128]{0:T(128)S(1)}, f32[128]{0:T(128)}, u32[]{:S(2)}) copy-start(f32[128]{0:T(128)} %param.14) | copy-start | bytes 1540
  29.7 149.9 %all-gather.2.cloned.1.call-start = ((), (), s32[]{:S(2)}) async-start(), calls=%async_computation.1 | async-start | bytes 9437184 | tf_op jit(solution)/shard_map/all_gather | solution.py:36
  88.2 1.8 copy-start.1
  132.6 1.2 copy-start.2
Sparse Core Ops, SparseCore 0:
  29.8 58.3 all-reduce.1
  134.0 45.5 all-gather.1
where the time goes:
time: 194 us
  waiting for transfers between devices  104 us (54%)
  matrix products  35.7 us (18%)
  blocking collectives  28 us (14%)
  between operations  14.2 us (7%)
  local copies, waits for them, and re-layouts  7.54 us (4%)
  other arithmetic  4.75 us (2%)
    psum x1, waiting for transfers between devices, device_step(): mlp_out = lax.psum(part_sum, 'tp')  58.4 us
    all_gather x1, waiting for transfers between devices, device_step(): log_probs = lax.all_gather(local_probs, 'tp', axis=1, tiled=True)  45.2 us
    dot_general x1, matrix products, device_step(): jnp.dot(hidden_act, w_down, preferred_element_type=jnp.float32)  14.7 us
    pmax x1, blocking collectives, device_step(): row_max = lax.pmax(jnp.max(logits, axis=-1), 'tp')  14.6 us
    psum x1, blocking collectives, device_step(): row_stats = lax.psum(local_stats, 'tp')  13.4 us
    dot_general x1, matrix products, device_step(): jnp.dot(normed, w_vocab, preferred_element_type=jnp.float32)  13.3 us
    dot_general x1, matrix products, device_step(): gate_pre = jnp.dot(hidden, w_gate, preferred_element_type=jnp.float32)  7.63 us
    unnamed x13, local copies, waits for them, and re-layouts  7.54 us
  transfers between devices with their start and end apart: 2, of which 2 were waited for; matrix products, arithmetic and copies ran while one was open for 0% of the time, Pallas kernels for 0%

commit v1 on v0

v1 whole, which is shorter than its diff:
```python
import functools

import jax
import jax.numpy as jnp
from jax import lax
from jax.experimental import pallas as pl
from jax.experimental.pallas import tpu as pltpu
from jax.sharding import PartitionSpec as P

NORM_EPS = 1e-6
MESH = pl.DeviceIdType.MESH
F32 = jnp.float32
BF16 = jnp.bfloat16

SLAB = 256
AHEAD = 3

ID_PART = 0
ID_ATOP, ID_ABOT, ID_BNXT, ID_BPRV = 4, 5, 6, 7
ID_YNXT, ID_YPRV, ID_YDIE = 8, 9, 10
ID_RNXT, ID_RPRV = 11, 12
ID_FPRV, ID_FNXT, ID_FTOP, ID_FBOT = 13, 14, 15, 16
ID_ZNXT = 17


def main_kernel(n, h_hbm, wg_hbm, wu_hbm, wd_hbm, gain_hbm, wv_hbm, temp_hbm, targ_hbm,
                z_ref, st_ref,
                wbuf, dbuf, h_ref, x_ref, a_ref, gain_ref, temp_ref, targ_ref,
                psend, prcv, abuf, arcv, bsend, brcv, chip_ref, ygat, cols_ref,
                ss, rs, wsem, dsem, msem):
    chips = n // 2
    rows, dim = h_ref.shape
    half = rows // 2
    f_loc = a_ref.shape[1]
    nf = f_loc // SLAB
    own_w = dim // n
    tile_w = z_ref.shape[2]
    tiles = z_ref.shape[0] // n
    per_tile = tile_w // SLAB
    id_zprv = ID_ZNXT + tiles
    id_zdie = id_zprv + tiles
    id_zrel = id_zdie + tiles
    id_zfp = id_zrel + tiles
    id_zfn = id_zfp + tiles
    id_zfo = id_zfn + tiles
    id_stat = id_zfo + tiles

    me = lax.axis_index("tp")
    chip, core = me // 2, me % 2
    other = 1 - core
    c_nxt, c_prv, c_opp = (chip + 1) % chips, (chip + chips - 1) % chips, (chip + 2) % chips
    nxt, prv, opp = c_nxt * 2 + core, c_prv * 2 + core, c_opp * 2 + core
    die = chip * 2 + other

    def remote(src, dst, k, dev):
        return pltpu.make_async_remote_copy(src_ref=src, dst_ref=dst, send_sem=ss.at[k], recv_sem=rs.at[k],
                                            device_id={"tp": dev}, device_id_type=MESH)

    small = [pltpu.make_async_copy(h_hbm, h_ref, msem.at[0]),
             pltpu.make_async_copy(gain_hbm, gain_ref, msem.at[1]),
             pltpu.make_async_copy(temp_hbm, temp_ref, msem.at[2]),
             pltpu.make_async_copy(targ_hbm, targ_ref, msem.at[3])]

    def gate_up(j):
        col = pl.ds(pl.multiple_of(j * SLAB, SLAB), SLAB)
        return (pltpu.make_async_copy(wg_hbm.at[:, col], wbuf.at[2 * j], wsem.at[2 * j]),
                pltpu.make_async_copy(wu_hbm.at[:, col], wbuf.at[2 * j + 1], wsem.at[2 * j + 1]))

    def vocab(s):
        col = pl.ds(pl.multiple_of(s * SLAB, SLAB), SLAB)
        return pltpu.make_async_copy(wv_hbm.at[:, col], wbuf.at[s], wsem.at[s])

    def down(k, dev):
        col = pl.ds(pl.multiple_of(dev * own_w, own_w), own_w)
        return pltpu.make_async_copy(wd_hbm.at[:, col], dbuf.at[k], dsem.at[k])

    order = []
    for target in (c_opp, c_nxt, c_prv, chip):
        order += [target * 2 + other, target * 2 + core]

    small[0].start()
    for j in range(AHEAD):
        for c in gate_up(j):
            c.start()
    for c in small[1:]:
        c.start()

    barrier = pltpu.get_barrier_semaphore()
    for r in range(1, n):
        pl.semaphore_signal(barrier, inc=1, device_id={"tp": (me + r) % n}, device_id_type=MESH)

    small[0].wait()

    @pl.loop(0, nf)
    def _(j):
        for c in gate_up(j):
            c.wait()

        @pl.when(j + AHEAD < nf)
        def _():
            for c in gate_up(j + AHEAD):
                c.start()

        @pl.when(j + AHEAD >= nf)
        def _():
            for k in range(AHEAD):
                @pl.when(j + AHEAD == nf + k)
                def _():
                    down(k, order[k]).start()

        gate = jnp.dot(h_ref[...], wbuf[2 * j], preferred_element_type=F32)
        up = jnp.dot(h_ref[...], wbuf[2 * j + 1], preferred_element_type=F32)
        a_ref[:, pl.ds(pl.multiple_of(j * SLAB, SLAB), SLAB)] = (jax.nn.silu(gate) * up).astype(BF16)

    for c in small[1:]:
        c.wait()
    row_ids = lax.broadcasted_iota(jnp.int32, (rows, rows), 0)
    lane_ids = lax.broadcasted_iota(jnp.int32, (rows, rows), 1)
    eye = row_ids == lane_ids
    inv_temp = 1.0 / jnp.sum(jnp.where(eye, temp_ref[...], 0.0), axis=1, keepdims=True)
    targ = jnp.sum(jnp.where(eye, targ_ref[...].astype(F32), 0.0), axis=1, keepdims=True)
    cols_ref[0] = jnp.broadcast_to(inv_temp, (rows, 128))
    cols_ref[1] = jnp.broadcast_to(targ, (rows, 128))

    pl.semaphore_wait(barrier, n - 1)

    copies = []
    for k in range(2 * chips):
        if k + AHEAD < 2 * chips:
            down(k + AHEAD, order[k + AHEAD]).start()
        else:
            per = (tiles * per_tile) // AHEAD
            first = (k + AHEAD - 2 * chips) * per
            last = tiles * per_tile if k == 2 * chips - 1 else first + per
            for s in range(first, last):
                vocab(s).start()
        down(k, order[k]).wait()
        part = jnp.dot(a_ref[...], dbuf[k], preferred_element_type=F32)
        q = k // 2
        to_die = remote(psend.at[q], prcv.at[q], ID_PART + q, die)
        if k % 2 == 0:
            psend[q] = part.astype(BF16)
            to_die.start()
            copies.append(to_die)
            continue
        to_die.wait_recv()
        total = part + prcv[q].astype(F32)
        if q == 0:
            abuf[...] = total.astype(BF16)
            top = remote(abuf.at[pl.ds(0, half)], arcv.at[0], ID_ATOP, nxt)
            bot = remote(abuf.at[pl.ds(half, half)], arcv.at[1], ID_ABOT, prv)
            top.start()
            bot.start()
            copies += [top, bot]
        elif q < 3:
            chip_ref[q - 1] = total
        if q == 2:
            top.wait_recv()
            bsend[0, :half] = (chip_ref[0, :half] + arcv[0].astype(F32)).astype(BF16)
            bsend[0, half:] = chip_ref[0, half:].astype(BF16)
            b_nxt = remote(bsend.at[0], brcv.at[0], ID_BNXT, nxt)
            b_nxt.start()
            bot.wait_recv()
            bsend[1, :half] = chip_ref[1, :half].astype(BF16)
            bsend[1, half:] = (chip_ref[1, half:] + arcv[1].astype(F32)).astype(BF16)
            b_prv = remote(bsend.at[1], brcv.at[1], ID_BPRV, prv)
            b_prv.start()
            copies += [b_nxt, b_prv]
    b_nxt.wait_recv()
    b_prv.wait_recv()
    ygat[me] = (total + brcv[0].astype(F32) + brcv[1].astype(F32)).astype(BF16)

    y_nxt = remote(ygat.at[me], ygat.at[me], ID_YNXT, nxt)
    y_prv = remote(ygat.at[me], ygat.at[me], ID_YPRV, prv)
    y_die = remote(ygat.at[me], ygat.at[me], ID_YDIE, die)
    for c in (y_nxt, y_prv, y_die):
        c.start()
    top_rows, bot_rows = pl.ds(0, half), pl.ds(half, half)
    remote(ygat.at[prv], ygat.at[prv], ID_YNXT, nxt).wait_recv()
    r_nxt = remote(ygat.at[prv, top_rows], ygat.at[prv, top_rows], ID_RNXT, nxt)
    f_prv = remote(ygat.at[prv], ygat.at[prv], ID_FPRV, die)
    r_nxt.start()
    f_prv.start()
    remote(ygat.at[nxt], ygat.at[nxt], ID_YPRV, prv).wait_recv()
    r_prv = remote(ygat.at[nxt, bot_rows], ygat.at[nxt, bot_rows], ID_RPRV, prv)
    f_nxt = remote(ygat.at[nxt], ygat.at[nxt], ID_FNXT, die)
    r_prv.start()
    f_nxt.start()

    def residual(s):
        col = pl.ds(pl.multiple_of(s * own_w, own_w), own_w)
        return col, h_ref[:, col].astype(F32) + ygat[s].astype(F32)

    def squares(s):
        _, r = residual(s)
        return jnp.sum(r * r, axis=1, keepdims=True)

    total_sq = squares(me) + squares(prv) + squares(nxt)
    remote(ygat.at[die], ygat.at[die], ID_YDIE, die).wait_recv()
    total_sq += squares(die)
    p_prv, p_nxt, p_opp = c_prv * 2 + other, c_nxt * 2 + other, c_opp * 2 + other
    remote(ygat.at[p_prv], ygat.at[p_prv], ID_FPRV, die).wait_recv()
    total_sq += squares(p_prv)
    remote(ygat.at[p_nxt], ygat.at[p_nxt], ID_FNXT, die).wait_recv()
    total_sq += squares(p_nxt)
    remote(ygat.at[opp, top_rows], ygat.at[opp, top_rows], ID_RNXT, nxt).wait_recv()
    f_top = remote(ygat.at[opp, top_rows], ygat.at[opp, top_rows], ID_FTOP, die)
    f_top.start()
    remote(ygat.at[opp, bot_rows], ygat.at[opp, bot_rows], ID_RPRV, prv).wait_recv()
    f_bot = remote(ygat.at[opp, bot_rows], ygat.at[opp, bot_rows], ID_FBOT, die)
    f_bot.start()
    total_sq += squares(opp)
    remote(ygat.at[p_opp, top_rows], ygat.at[p_opp, top_rows], ID_FTOP, die).wait_recv()
    remote(ygat.at[p_opp, bot_rows], ygat.at[p_opp, bot_rows], ID_FBOT, die).wait_recv()
    total_sq += squares(p_opp)
    copies += [y_nxt, y_prv, y_die, r_nxt, r_prv, f_prv, f_nxt, f_top, f_bot]
    inv_rms = lax.rsqrt(total_sq * (1.0 / dim) + NORM_EPS)

    @pl.loop(0, n)
    def _(s):
        col, r = residual(s)
        x_ref[:, col] = (gain_ref[:, col] * r * inv_rms).astype(BF16)

    cols_ref[2] = jnp.zeros((rows, 128), F32)
    lanes = lax.broadcasted_iota(jnp.int32, (rows, 128), 1)

    def own_sends(t):
        blk = z_ref.at[me * tiles + t]
        return (remote(blk, blk, ID_ZNXT + t, nxt), remote(blk, blk, id_zprv + t, prv),
                remote(blk, blk, id_zdie + t, die))

    @pl.loop(0, tiles)
    def _(t):
        for i in range(per_tile):
            vocab(t * per_tile + i).wait()
        pieces = [jnp.dot(x_ref[...], wbuf[t * per_tile + i], preferred_element_type=F32) for i in range(per_tile)]
        logits = jnp.concatenate(pieces, axis=1) * cols_ref[0][:, :1]
        top_l = jnp.max(logits, axis=1, keepdims=True)
        low = logits - top_l
        z_ref[me * tiles + t] = low.astype(BF16)
        for c in own_sends(t):
            c.start()
        e = jnp.exp(low)
        ids = lax.broadcasted_iota(jnp.int32, (rows, tile_w), 1) + (me * tiles + t) * tile_w
        hit = jnp.where(ids.astype(F32) == cols_ref[1][:, :1], logits, 0.0)
        stats = cols_ref[2]
        for i, col in enumerate((top_l, jnp.sum(e, axis=1, keepdims=True), jnp.sum(e * logits, axis=1, keepdims=True),
                                 jnp.sum(hit, axis=1, keepdims=True))):
            stats = jnp.where(lanes == i * tiles + t, col, stats)
        cols_ref[2] = stats

    st_ref[me] = cols_ref[2].T[:4 * tiles]
    stat_sends = [remote(st_ref.at[me], st_ref.at[me], id_stat + r - 1, (me + r) % n) for r in range(1, n)]
    for c in stat_sends:
        c.start()
    copies += stat_sends

    def blk(dev, t):
        return z_ref.at[dev * tiles + t]

    for t in range(tiles):
        copies += own_sends(t)
        remote(blk(prv, t), blk(prv, t), ID_ZNXT + t, nxt).wait_recv()
        if t % 2 == 0:
            rel = remote(blk(prv, t), blk(prv, t), id_zrel + t, nxt)
            rel.start()
            copies.append(rel)
        fwd = remote(blk(prv, t), blk(prv, t), id_zfp + t, die)
        fwd.start()
        copies.append(fwd)
        remote(blk(nxt, t), blk(nxt, t), id_zprv + t, prv).wait_recv()
        if t % 2 == 1:
            rel = remote(blk(nxt, t), blk(nxt, t), id_zrel + t, prv)
            rel.start()
            copies.append(rel)
        fwd = remote(blk(nxt, t), blk(nxt, t), id_zfn + t, die)
        fwd.start()
        copies.append(fwd)
    for t in range(tiles):
        remote(blk(opp, t), blk(opp, t), id_zrel + t, nxt if t % 2 == 0 else prv).wait_recv()
        fwd = remote(blk(opp, t), blk(opp, t), id_zfo + t, die)
        fwd.start()
        copies.append(fwd)
    for t in range(tiles):
        remote(blk(die, t), blk(die, t), id_zdie + t, die).wait_recv()
        remote(blk(p_prv, t), blk(p_prv, t), id_zfp + t, die).wait_recv()
        remote(blk(p_nxt, t), blk(p_nxt, t), id_zfn + t, die).wait_recv()
    for t in range(tiles):
        remote(blk(p_opp, t), blk(p_opp, t), id_zfo + t, die).wait_recv()
    for r in range(1, n):
        src = (me + n - r) % n
        remote(st_ref.at[src], st_ref.at[src], id_stat + r - 1, src).wait_recv()
    for c in copies:
        c.wait_send()


def finish_kernel(z_ref, st_ref, norm_ref, ent_ref, logp_ref, out_hbm, d_ref, obuf, sem):
    blocks, rows, width = z_ref.shape
    n, four_t, _ = st_ref.shape
    tiles = four_t // 4
    top = jnp.max(jnp.max(st_ref[:, :tiles], axis=0), axis=0, keepdims=True)
    scale = jnp.exp(st_ref[:, :tiles] - top[None])

    def total(v):
        return jnp.sum(jnp.sum(v, axis=0), axis=0, keepdims=True)

    sum_exp = total(st_ref[:, tiles:2 * tiles] * scale)
    weighted = total(st_ref[:, 2 * tiles:3 * tiles] * scale)
    target_logit = total(st_ref[:, 3 * tiles:])
    log_norm = top + jnp.log(sum_exp)
    norm_ref[...] = log_norm
    ent_ref[...] = log_norm - weighted / sum_exp
    logp_ref[...] = target_logit - log_norm
    for dev in range(n):
        d_ref[dev] = jnp.concatenate([st_ref[dev, :tiles] - log_norm,
                                      jnp.zeros((128 - tiles, rows), F32)], axis=0).T

    def put(dev, t):
        b = dev * tiles + t
        return pltpu.make_async_copy(
            obuf.at[b], out_hbm.at[:, pl.ds(pl.multiple_of(b * width, width), width)], sem.at[b])

    @pl.loop(0, n)
    def _(dev):
        shift = d_ref[dev]
        for t in range(tiles):
            obuf[dev * tiles + t] = (z_ref[dev * tiles + t].astype(F32) + shift[:, t:t + 1]).astype(BF16)
            put(dev, t).start()

    @pl.loop(0, n)
    def _(dev):
        for t in range(tiles):
            put(dev, t).wait()


def solution(mesh):
    n = mesh.shape["tp"]

    def device_step(hidden, w_gate, w_up, w_down, norm_gain, w_vocab, temperature, target):
        rows, dim = hidden.shape
        f_loc = w_gate.shape[1]
        v_loc = w_vocab.shape[1]
        own_w = dim // n
        tile_w = 512
        tiles = v_loc // tile_w
        n_ids = ID_ZNXT + 7 * tiles + n
        any_spec = pl.BlockSpec(memory_space=pl.ANY)
        vmem = pl.BlockSpec(memory_space=pltpu.VMEM)
        z, stats = pl.pallas_call(
            functools.partial(main_kernel, n),
            out_shape=(pltpu.VMEM((n * tiles, rows, tile_w), BF16), pltpu.VMEM((n, 4 * tiles, rows), F32)),
            in_specs=[any_spec] * 8,
            out_specs=(vmem, vmem),
            scratch_shapes=[
                pltpu.VMEM((v_loc // SLAB, dim, SLAB), BF16),
                pltpu.VMEM((n, f_loc, own_w), BF16),
                pltpu.VMEM((rows, dim), BF16),
                pltpu.VMEM((rows, dim), BF16),
                pltpu.VMEM((rows, f_loc), BF16),
                pltpu.VMEM((1, dim), F32),
                pltpu.VMEM((1, rows), F32),
                pltpu.VMEM((1, rows), jnp.int32),
                pltpu.VMEM((4, rows, own_w), BF16),
                pltpu.VMEM((4, rows, own_w), BF16),
                pltpu.VMEM((rows, own_w), BF16),
                pltpu.VMEM((2, rows // 2, own_w), BF16),
                pltpu.VMEM((2, rows, own_w), BF16),
                pltpu.VMEM((2, rows, own_w), BF16),
                pltpu.VMEM((2, rows, own_w), F32),
                pltpu.VMEM((n, rows, own_w), BF16),
                pltpu.VMEM((3, rows, 128), F32),
                pltpu.SemaphoreType.DMA((n_ids,)),
                pltpu.SemaphoreType.DMA((n_ids,)),
                pltpu.SemaphoreType.DMA((v_loc // SLAB,)),
                pltpu.SemaphoreType.DMA((n,)),
                pltpu.SemaphoreType.DMA((4,)),
            ],
            compiler_params=pltpu.CompilerParams(
                collective_id=0, has_side_effects=True, vmem_limit_bytes=55 * 1024 * 1024),
            name="decode_tail",
        )(hidden, w_gate, w_up, w_down, norm_gain.reshape(1, dim), w_vocab, temperature.reshape(1, rows),
          target.reshape(1, rows))
        row = jax.ShapeDtypeStruct((1, rows), F32)
        log_norm, entropy, target_logp, log_probs = pl.pallas_call(
            finish_kernel,
            out_shape=(row, row, row, jax.ShapeDtypeStruct((rows, n * v_loc), BF16)),
            in_specs=[vmem, vmem],
            out_specs=(vmem, vmem, vmem, any_spec),
            scratch_shapes=[
                pltpu.VMEM((n, rows, 128), F32),
                pltpu.VMEM((n * tiles, rows, tile_w), BF16),
                pltpu.SemaphoreType.DMA((n * tiles,)),
            ],
            compiler_params=pltpu.CompilerParams(vmem_limit_bytes=24 * 1024 * 1024),
            name="write_log_probs",
        )(z, stats)
        return log_norm.reshape(rows), entropy.reshape(rows), target_logp.reshape(rows), log_probs

    return jax.shard_map(
        device_step,
        mesh=mesh,
        in_specs=(P("dp", None), P(None, "tp"), P(None, "tp"), P("tp", None), P(None),
                  P(None, "tp"), P("dp"), P("dp")),
        out_specs=(P("dp"), P("dp"), P("dp"), P("dp", None)),
        check_vma=False,
    )
```

time: 194 us -> 81.7 us (0.42)
  waiting for transfers between devices: 104 us -> 0 us
  Pallas kernels: 0 us -> 80.9 us
  matrix products: 35.7 us -> 0 us
  blocking collectives: 28 us -> 0 us
  between operations: 14.2 us -> 0.64 us
  local copies, waits for them, and re-layouts: 7.54 us -> 0 us
  other arithmetic: 4.75 us -> 0 us
    pallas_call x0 -> x2, Pallas kernels: none -> 80.9 us  [the longest x1 76.3 us: device_step(): pl.pallas_call(functools.partial(main_kernel, n), out_shape=(pltpu.VMEM((...]
    psum x1 -> x0, waiting for transfers between devices: 58.4 us -> none  [device_step(): mlp_out = lax.psum(part_sum, 'tp')]
    all_gather x1 -> x0, waiting for transfers between devices: 45.2 us -> none  [device_step(): log_probs = lax.all_gather(local_probs, 'tp', axis=1, tiled=True)]
    dot_general x3 -> x0, matrix products: 35.7 us -> none  [the longest x1 14.7 us: device_step(): jnp.dot(hidden_act, w_down, preferred_element_type=jnp.float32)]
    pmax x1 -> x0, blocking collectives: 14.6 us -> none  [device_step(): row_max = lax.pmax(jnp.max(logits, axis=-1), 'tp')]
    psum x1 -> x0, blocking collectives: 13.4 us -> none  [device_step(): row_stats = lax.psum(local_stats, 'tp')]
    unnamed x13 -> x0, local copies, waits for them, and re-layouts: 7.54 us -> none
    reduce_sum x2 -> x0, other arithmetic: 2.5 us -> none  [the longest x1 1.73 us: device_step(): jnp.mean(residual * residual, axis=-1, keepdims=True) + NORM_EPS]
  transfers between devices with their start and end apart: 2 -> 0, of which waited for: 2 -> 0; matrix products, arithmetic and copies ran while one was open for 0% -> 0% of each run, Pallas kernels for 0% -> 0%
where the time goes in v1:
time: 81.7 us; the launch traced here: 81.6 us
  Pallas kernels  80.9 us (99%)
    pallas_call x1, Pallas kernels, device_step(): pl.pallas_call(functools.partial(main_kernel, n), out_shape=(pltpu.VMEM((...  76.3 us
    pallas_call x1, Pallas kernels, device_step(): pl.pallas_call(finish_kernel, out_shape=(row, row, row, jax.ShapeDtypeStr...  4.66 us

profile of v1, /device:TPU:81, one launch (start us, length us, event | category | flops | bytes accessed | tf_op | source)
XLA Modules:
  0.0 81.6 jit_solution(9686181387646407416)
XLA Ops:
  0.6 76.3 %decode_tail.1 = (bf16[64,128,512]{2,1,0:T(8,128)(2,1)S(1)}, f32[8,32,128]{2,1,0:T(8,128)S(1)}) custom-call(bf16[128,4096]{1,0:T(8,128)(2,1)} %h_hbm.1, bf16[4096,1792]{1,0:T(8,128)(2,1)} %wg_hbm.1, bf16[4096,1792]{1,0:T(8,128)(2,1)} %wu_hbm.1, bf16[1792,4096]{1,0:T(8,128)(2,1)} %wd_hbm.1, f32[1,4096]{1,0:T(1,128)} %bitcast.6, bf16[4096,4096]{1,0:T(8,128)(2,1)} %wv_hbm.1, ...), custom_call_target="tpu_custom_call" | custom-call | tf_op jit(solution)/shard_map/decode_tail/pallas_call | solution.py:349
  76.9 4.7 %write_log_probs.1 = (f32[1,128]{1,0:T(1,128)}, f32[1,128]{1,0:T(1,128)}, f32[1,128]{1,0:T(1,128)}, bf16[128,32768]{1,0:T(8,128)(2,1)}) custom-call(bf16[64,128,512]{2,1,0:T(8,128)(2,1)S(1)} %get-tuple-element.10.z_ref, f32[8,32,128]{2,1,0:T(8,128)S(1)} %get-tuple-element.11.st_ref), custom_call_target="tpu_custom_call" | custom-call | tf_op jit(solution)/shard_map/write_log_probs/pallas_call | solution.py:384

commit v2 on v0

v2 whole, which is shorter than its diff:
```python
import functools

import jax
import jax.numpy as jnp
from jax import lax
from jax.experimental import pallas as pl
from jax.experimental.pallas import tpu as pltpu
from jax.sharding import PartitionSpec as P

NORM_EPS = 1e-6
MESH = pl.DeviceIdType.MESH
F32 = jnp.float32
BF16 = jnp.bfloat16

SLAB = 256
AHEAD = 3
DOWN_AHEAD = 3
DOWN_SLOTS = 5
GROUPS = 2
TILE = 512
EARLY = 4


class Ids:
    def __init__(self, chips, tiles):
        self.count = 0
        g = GROUPS
        self.part = self.take(chips)
        self.atop, self.abot, self.bnxt, self.bprv = (self.take(g) for _ in range(4))
        self.ynxt, self.yprv, self.ydie = (self.take(g) for _ in range(3))
        self.rnxt, self.rprv, self.fprv, self.fnxt, self.ftop, self.fbot = (self.take(g) for _ in range(6))
        self.znxt, self.zprv, self.zdie, self.zrel, self.zfp, self.zfn, self.zfo = (
            self.take(g * tiles) for _ in range(7))
        self.snxt, self.sprv, self.sopp, self.sdie, self.sfp, self.sfn, self.sfo = (self.take(1) for _ in range(7))

    def take(self, k):
        first = self.count
        self.count += k
        return first


def main_kernel(n, h_hbm, wg_hbm, wu_hbm, wd_hbm, gain_hbm, wv_hbm, temp_hbm, targ_hbm,
                z_ref, fin_ref,
                wbuf, dbuf, h_ref, x_ref, a_ref, gain_ref, temp_ref, targ_ref,
                psend, prcv, abuf, arcv, bsend, brcv, chip_ref, ygat, cols_ref, st_ref, shift_ref,
                ss, rs, wsem, dsem, msem):
    chips = n // 2
    rows, dim = h_ref.shape
    grp = rows // GROUPS
    half = grp // 2
    kh = dim // 2
    f_loc = a_ref.shape[1]
    nf = f_loc // SLAB
    own_w = dim // n
    tiles = z_ref.shape[0] // n
    per_tile = TILE // SLAB
    ids = Ids(chips, tiles)

    me = lax.axis_index("tp")
    chip, core = me // 2, me % 2
    other = 1 - core
    c_nxt, c_prv, c_opp = (chip + 1) % chips, (chip + chips - 1) % chips, (chip + 2) % chips
    nxt, prv, opp = c_nxt * 2 + core, c_prv * 2 + core, c_opp * 2 + core
    die = chip * 2 + other
    p_prv, p_nxt, p_opp = c_prv * 2 + other, c_nxt * 2 + other, c_opp * 2 + other

    def remote(src, dst, k, dev):
        return pltpu.make_async_remote_copy(src_ref=src, dst_ref=dst, send_sem=ss.at[k], recv_sem=rs.at[k],
                                            device_id={"tp": dev}, device_id_type=MESH)

    copies = []

    def send(ref, k, dev):
        c = remote(ref, ref, k, dev)
        c.start()
        copies.append(c)
        return c

    def arrived(ref, k):
        remote(ref, ref, k, die).wait_recv()

    def g_rows(g):
        return pl.ds(g * grp, grp)

    def g_top(g):
        return pl.ds(g * grp, half)

    def g_bot(g):
        return pl.ds(g * grp + half, half)

    small = [pltpu.make_async_copy(h_hbm, h_ref, msem.at[0]),
             pltpu.make_async_copy(gain_hbm, gain_ref, msem.at[1]),
             pltpu.make_async_copy(temp_hbm, temp_ref, msem.at[2]),
             pltpu.make_async_copy(targ_hbm, targ_ref, msem.at[3])]

    def gate_up(j, part):
        col = pl.ds(pl.multiple_of(j * SLAB, SLAB), SLAB)
        k = pl.ds(part * kh, kh)
        return (pltpu.make_async_copy(wg_hbm.at[k, col], wbuf.at[2 * j, k], wsem.at[2 * part, j]),
                pltpu.make_async_copy(wu_hbm.at[k, col], wbuf.at[2 * j + 1, k], wsem.at[2 * part + 1, j]))

    def start_gate_up(j):
        for part in range(2):
            for c in gate_up(j, part):
                c.start()

    def vocab(s):
        col = pl.ds(pl.multiple_of(s * SLAB, SLAB), SLAB)
        return pltpu.make_async_copy(wv_hbm.at[:, col], wbuf.at[s], wsem.at[4, s])

    def down(k, dev):
        col = pl.ds(pl.multiple_of(dev * own_w, own_w), own_w)
        return pltpu.make_async_copy(wd_hbm.at[:, col], dbuf.at[k % DOWN_SLOTS], dsem.at[k])

    plan = ((c_opp, 0, True), (c_nxt, 1, True), (c_opp, 0, False), (c_prv, 2, True),
            (c_nxt, 1, False), (chip, 3, True), (c_prv, 2, False), (chip, 3, False))
    order = [c * 2 + (other if away else core) for c, _, away in plan]

    small[0].start()
    for j in range(AHEAD):
        start_gate_up(j)
    for c in small[1:]:
        c.start()

    barrier = pltpu.get_barrier_semaphore()
    for r in range(1, n):
        pl.semaphore_signal(barrier, inc=1, device_id={"tp": (me + r) % n}, device_id_type=MESH)

    small[0].wait()

    @pl.loop(0, nf)
    def _(j):
        for c in gate_up(j, 0):
            c.wait()

        @pl.when(j + AHEAD < nf)
        def _():
            start_gate_up(j + AHEAD)

        for k in range(DOWN_AHEAD):
            @pl.when(j == nf - AHEAD + min(k, AHEAD - 1))
            def _():
                down(k, order[k]).start()

        h0 = h_ref[:, :kh]
        gate = jnp.dot(h0, wbuf[2 * j, :kh], preferred_element_type=F32)
        up = jnp.dot(h0, wbuf[2 * j + 1, :kh], preferred_element_type=F32)
        for c in gate_up(j, 1):
            c.wait()
        h1 = h_ref[:, kh:]
        gate += jnp.dot(h1, wbuf[2 * j, kh:], preferred_element_type=F32)
        up += jnp.dot(h1, wbuf[2 * j + 1, kh:], preferred_element_type=F32)
        a_ref[:, pl.ds(pl.multiple_of(j * SLAB, SLAB), SLAB)] = (jax.nn.silu(gate) * up).astype(BF16)

    n_down = len(plan)
    for k, (_, q, away) in enumerate(plan):
        if k + DOWN_AHEAD < n_down:
            down(k + DOWN_AHEAD, order[k + DOWN_AHEAD]).start()
        else:
            per = (tiles * per_tile) // DOWN_AHEAD
            first = (k + DOWN_AHEAD - n_down) * per
            last = tiles * per_tile if k == n_down - 1 else first + per
            for s in range(first, last):
                vocab(s).start()
        down(k, order[k]).wait()
        part = jnp.dot(a_ref[...], dbuf[k % DOWN_SLOTS], preferred_element_type=F32)
        to_die = remote(psend.at[q], prcv.at[q], ids.part + q, die)
        if k == 0:
            pl.semaphore_wait(barrier, n - 1)
        if away:
            psend[q] = part.astype(BF16)
            to_die.start()
            copies.append(to_die)
            continue
        to_die.wait_recv()
        total = part + prcv[q].astype(F32)
        if q == 0:
            abuf[...] = total.astype(BF16)
            for g in range(GROUPS):
                for rws, k_id, dev in ((g_top(g), ids.atop, nxt), (g_bot(g), ids.abot, prv)):
                    c = remote(abuf.at[rws], arcv.at[rws], k_id + g, dev)
                    c.start()
                    copies.append(c)
        else:
            chip_ref[q - 1] = total

    for g in range(GROUPS):
        t_sl, b_sl = slice(g * grp, g * grp + half), slice(g * grp + half, (g + 1) * grp)
        arrived(arcv.at[g_top(g)], ids.atop + g)
        bsend[0, t_sl] = (chip_ref[0, t_sl] + arcv[t_sl].astype(F32)).astype(BF16)
        bsend[0, b_sl] = chip_ref[0, b_sl].astype(BF16)
        c = remote(bsend.at[0, g_rows(g)], brcv.at[0, g_rows(g)], ids.bnxt + g, nxt)
        c.start()
        copies.append(c)
        arrived(arcv.at[g_bot(g)], ids.abot + g)
        bsend[1, t_sl] = chip_ref[1, t_sl].astype(BF16)
        bsend[1, b_sl] = (chip_ref[1, b_sl] + arcv[b_sl].astype(F32)).astype(BF16)
        c = remote(bsend.at[1, g_rows(g)], brcv.at[1, g_rows(g)], ids.bprv + g, prv)
        c.start()
        copies.append(c)

    for c in small[1:]:
        c.wait()
    row_ids = lax.broadcasted_iota(jnp.int32, (rows, rows), 0)
    lane_ids = lax.broadcasted_iota(jnp.int32, (rows, rows), 1)
    eye = row_ids == lane_ids
    inv_temp = 1.0 / jnp.sum(jnp.where(eye, temp_ref[...], 0.0), axis=1, keepdims=True)
    targ = jnp.sum(jnp.where(eye, targ_ref[...].astype(F32), 0.0), axis=1, keepdims=True)
    cols_ref[0] = jnp.broadcast_to(inv_temp, (rows, 128))
    cols_ref[1] = jnp.broadcast_to(targ, (rows, 128))
    cols_ref[2] = jnp.zeros((rows, 128), F32)

    for g in range(GROUPS):
        g_sl = slice(g * grp, (g + 1) * grp)
        arrived(brcv.at[0, g_rows(g)], ids.bnxt + g)
        arrived(brcv.at[1, g_rows(g)], ids.bprv + g)
        ygat[me, g_sl] = (chip_ref[2, g_sl] + brcv[0, g_sl].astype(F32) + brcv[1, g_sl].astype(F32)).astype(BF16)
        own = ygat.at[me, g_rows(g)]
        send(own, ids.ynxt + g, nxt)
        send(own, ids.yprv + g, prv)
        send(own, ids.ydie + g, die)
    for g in range(GROUPS):
        arrived(ygat.at[prv, g_rows(g)], ids.ynxt + g)
        send(ygat.at[prv, g_top(g)], ids.rnxt + g, nxt)
        send(ygat.at[prv, g_rows(g)], ids.fprv + g, die)
        arrived(ygat.at[nxt, g_rows(g)], ids.yprv + g)
        send(ygat.at[nxt, g_bot(g)], ids.rprv + g, prv)
        send(ygat.at[nxt, g_rows(g)], ids.fnxt + g, die)

    def residual(s, g):
        col = pl.ds(pl.multiple_of(s * own_w, own_w), own_w)
        return col, h_ref[g_rows(g), col].astype(F32) + ygat[s, g * grp:(g + 1) * grp].astype(F32)

    def squares(s, g):
        _, r = residual(s, g)
        return jnp.sum(r * r, axis=1, keepdims=True)

    def finish_sum(g):
        arrived(ygat.at[opp, g_top(g)], ids.rnxt + g)
        send(ygat.at[opp, g_top(g)], ids.ftop + g, die)
        arrived(ygat.at[opp, g_bot(g)], ids.rprv + g)
        send(ygat.at[opp, g_bot(g)], ids.fbot + g, die)

    def normalize(g):
        total_sq = squares(me, g) + squares(prv, g) + squares(nxt, g) + squares(opp, g)
        for s, k in ((die, ids.ydie), (p_prv, ids.fprv), (p_nxt, ids.fnxt)):
            arrived(ygat.at[s, g_rows(g)], k + g)
            total_sq += squares(s, g)
        arrived(ygat.at[p_opp, g_top(g)], ids.ftop + g)
        arrived(ygat.at[p_opp, g_bot(g)], ids.fbot + g)
        total_sq += squares(p_opp, g)
        inv_rms = lax.rsqrt(total_sq * (1.0 / dim) + NORM_EPS)

        @pl.loop(0, n)
        def _(s):
            col, r = residual(s, g)
            x_ref[g_rows(g), col] = (gain_ref[:, col] * r * inv_rms).astype(BF16)

    lanes = lax.broadcasted_iota(jnp.int32, (grp, 128), 1)

    def blk(dev, t, g):
        return z_ref.at[dev * tiles + t, g_rows(g)]

    def own_sends(t, g):
        b = blk(me, t, g)
        at = g * tiles + t
        return (remote(b, b, ids.znxt + at, nxt), remote(b, b, ids.zprv + at, prv), remote(b, b, ids.zdie + at, die))

    def head(g, t0, t1):
        sl = slice(g * grp, (g + 1) * grp)

        @pl.loop(t0, t1)
        def _(t):
            if g == 0:
                for i in range(per_tile):
                    vocab(t * per_tile + i).wait()
            pieces = [jnp.dot(x_ref[sl], wbuf[t * per_tile + i], preferred_element_type=F32) for i in range(per_tile)]
            logits = jnp.concatenate(pieces, axis=1) * cols_ref[0, sl][:, :1]
            top_l = jnp.max(logits, axis=1, keepdims=True)
            low = logits - top_l
            z_ref[me * tiles + t, sl] = low.astype(BF16)
            for c in own_sends(t, g):
                c.start()
            e = jnp.exp(low)
            col_ids = lax.broadcasted_iota(jnp.int32, (grp, TILE), 1) + (me * tiles + t) * TILE
            hit = jnp.where(col_ids.astype(F32) == cols_ref[1, sl][:, :1], logits, 0.0)
            stats = cols_ref[2, sl]
            for i, col in enumerate((top_l, jnp.sum(e, axis=1, keepdims=True),
                                     jnp.sum(e * logits, axis=1, keepdims=True), jnp.sum(hit, axis=1, keepdims=True))):
                stats = jnp.where(lanes == i * tiles + t, col, stats)
            cols_ref[2, sl] = stats

    finish_sum(0)
    normalize(0)
    for g in range(GROUPS):
        head(g, 0, EARLY)
        if g + 1 < GROUPS:
            finish_sum(g + 1)
        head(g, EARLY, tiles)
        if g + 1 < GROUPS:
            normalize(g + 1)

    by_row = cols_ref[2].T
    tops = by_row[:tiles]
    scale = jnp.exp(tops - jnp.max(tops, axis=0, keepdims=True))
    st_ref[me] = jnp.concatenate(
        [tops, jnp.sum(by_row[tiles:2 * tiles] * scale, axis=0, keepdims=True),
         jnp.sum(by_row[2 * tiles:3 * tiles] * scale, axis=0, keepdims=True),
         jnp.sum(by_row[3 * tiles:4 * tiles], axis=0, keepdims=True),
         jnp.zeros((st_ref.shape[1] - tiles - 3, rows), F32)], axis=0)
    send(st_ref.at[me], ids.snxt, nxt)
    send(st_ref.at[me], ids.sprv, prv)
    send(st_ref.at[me], ids.sopp, opp)
    send(st_ref.at[me], ids.sdie, die)

    sent = {}
    for g in range(GROUPS):
        for t in range(tiles):
            at = g * tiles + t
            sent["me", t, g] = list(own_sends(t, g))
            arrived(blk(prv, t, g), ids.znxt + at)
            sent["prv", t, g] = []
            sent["nxt", t, g] = []
            if t % 2 == 0:
                sent["prv", t, g].append(send(blk(prv, t, g), ids.zrel + at, nxt))
            sent["prv", t, g].append(send(blk(prv, t, g), ids.zfp + at, die))
            arrived(blk(nxt, t, g), ids.zprv + at)
            if t % 2 == 1:
                sent["nxt", t, g].append(send(blk(nxt, t, g), ids.zrel + at, prv))
            sent["nxt", t, g].append(send(blk(nxt, t, g), ids.zfn + at, die))

    arrived(st_ref.at[prv], ids.snxt)
    send(st_ref.at[prv], ids.sfp, die)
    arrived(st_ref.at[nxt], ids.sprv)
    send(st_ref.at[nxt], ids.sfn, die)
    arrived(st_ref.at[opp], ids.sopp)
    send(st_ref.at[opp], ids.sfo, die)
    for s, k in ((die, ids.sdie), (p_prv, ids.sfp), (p_nxt, ids.sfn), (p_opp, ids.sfo)):
        arrived(st_ref.at[s], k)

    dev_top = jnp.max(st_ref[:, :tiles], axis=1)
    top = jnp.max(dev_top, axis=0, keepdims=True)
    scale = jnp.exp(dev_top - top)
    sum_exp = jnp.sum(st_ref[:, tiles] * scale, axis=0, keepdims=True)
    weighted = jnp.sum(st_ref[:, tiles + 1] * scale, axis=0, keepdims=True)
    target_logit = jnp.sum(st_ref[:, tiles + 2], axis=0, keepdims=True)
    log_norm = top + jnp.log(sum_exp)
    fin_ref[0:1] = log_norm
    fin_ref[1:2] = log_norm - weighted / sum_exp
    fin_ref[2:3] = target_logit - log_norm
    pad = jnp.zeros((128 - tiles, rows), F32)

    @pl.loop(0, n)
    def _(dev):
        shift_ref[dev] = jnp.concatenate([st_ref[dev, :tiles] - log_norm, pad], axis=0).T

    done = set()

    def correct(name, dev, t):
        for g in range(GROUPS):
            for c in sent.get((name, t, g), ()):
                c.wait_send()
                done.add(id(c))
        b = dev * tiles + t
        z_ref[b] = (z_ref[b].astype(F32) + shift_ref[dev][:, t:t + 1]).astype(BF16)

    ready = []
    for t in range(tiles):
        ready += [("me", me, t), ("prv", prv, t), ("nxt", nxt, t), ("die", die, t), ("p_prv", p_prv, t), ("p_nxt", p_nxt, t)]
    landed = {"die": ids.zdie, "p_prv": ids.zfp, "p_nxt": ids.zfn, "p_opp": ids.zfo}

    def settle(name, dev, t):
        if name in landed:
            for g in range(GROUPS):
                arrived(blk(dev, t, g), landed[name] + g * tiles + t)
        correct(name, dev, t)

    steps = GROUPS * tiles
    taken = 0
    for g in range(GROUPS):
        for t in range(tiles):
            at = g * tiles + t
            upto = (at * len(ready)) // (steps - 1)
            for item in ready[taken:upto]:
                settle(*item)
            taken = max(taken, upto)
            arrived(blk(opp, t, g), ids.zrel + at)
            sent["opp", t, g] = [send(blk(opp, t, g), ids.zfo + at, die)]
            if g == GROUPS - 1 and t > 0:
                settle("opp", opp, t - 1)
                settle("p_opp", p_opp, t - 1)
    settle("opp", opp, tiles - 1)
    settle("p_opp", p_opp, tiles - 1)
    for c in copies:
        if id(c) not in done:
            c.wait_send()


def finish_kernel(z_ref, fin_ref, norm_ref, ent_ref, logp_ref, out_hbm, sem):
    blocks, rows, width = z_ref.shape

    def put(b):
        return pltpu.make_async_copy(
            z_ref.at[b], out_hbm.at[:, pl.ds(pl.multiple_of(b * width, width), width)], sem.at[b])

    @pl.loop(0, blocks)
    def _(b):
        put(b).start()

    norm_ref[...] = fin_ref[0:1]
    ent_ref[...] = fin_ref[1:2]
    logp_ref[...] = fin_ref[2:3]

    @pl.loop(0, blocks)
    def _(b):
        put(b).wait()


def solution(mesh):
    n = mesh.shape["tp"]

    def device_step(hidden, w_gate, w_up, w_down, norm_gain, w_vocab, temperature, target):
        rows, dim = hidden.shape
        f_loc = w_gate.shape[1]
        v_loc = w_vocab.shape[1]
        own_w = dim // n
        tiles = v_loc // TILE
        n_ids = Ids(n // 2, tiles).count
        any_spec = pl.BlockSpec(memory_space=pl.ANY)
        vmem = pl.BlockSpec(memory_space=pltpu.VMEM)
        z, fin = pl.pallas_call(
            functools.partial(main_kernel, n),
            out_shape=(pltpu.VMEM((n * tiles, rows, TILE), BF16), pltpu.VMEM((8, rows), F32)),
            in_specs=[any_spec] * 8,
            out_specs=(vmem, vmem),
            scratch_shapes=[
                pltpu.VMEM((v_loc // SLAB, dim, SLAB), BF16),
                pltpu.VMEM((DOWN_SLOTS, f_loc, own_w), BF16),
                pltpu.VMEM((rows, dim), BF16),
                pltpu.VMEM((rows, dim), BF16),
                pltpu.VMEM((rows, f_loc), BF16),
                pltpu.VMEM((1, dim), F32),
                pltpu.VMEM((1, rows), F32),
                pltpu.VMEM((1, rows), jnp.int32),
                pltpu.VMEM((4, rows, own_w), BF16),
                pltpu.VMEM((4, rows, own_w), BF16),
                pltpu.VMEM((rows, own_w), BF16),
                pltpu.VMEM((rows, own_w), BF16),
                pltpu.VMEM((2, rows, own_w), BF16),
                pltpu.VMEM((2, rows, own_w), BF16),
                pltpu.VMEM((3, rows, own_w), F32),
                pltpu.VMEM((n, rows, own_w), BF16),
                pltpu.VMEM((3, rows, 128), F32),
                pltpu.VMEM((n, 16, rows), F32),
                pltpu.VMEM((n, rows, 128), F32),
                pltpu.SemaphoreType.DMA((n_ids,)),
                pltpu.SemaphoreType.DMA((n_ids,)),
                pltpu.SemaphoreType.DMA((5, v_loc // SLAB)),
                pltpu.SemaphoreType.DMA((n,)),
                pltpu.SemaphoreType.DMA((4,)),
            ],
            compiler_params=pltpu.CompilerParams(
                collective_id=0, has_side_effects=True, vmem_limit_bytes=55 * 1024 * 1024),
            name="decode_tail",
        )(hidden, w_gate, w_up, w_down, norm_gain.reshape(1, dim), w_vocab, temperature.reshape(1, rows),
          target.reshape(1, rows))
        row = jax.ShapeDtypeStruct((1, rows), F32)
        log_norm, entropy, target_logp, log_probs = pl.pallas_call(
            finish_kernel,
            out_shape=(row, row, row, jax.ShapeDtypeStruct((rows, n * v_loc), BF16)),
            in_specs=[vmem, vmem],
            out_specs=(vmem, vmem, vmem, any_spec),
            scratch_shapes=[pltpu.SemaphoreType.DMA((n * tiles,))],
            compiler_params=pltpu.CompilerParams(vmem_limit_bytes=4 * 1024 * 1024),
            name="write_log_probs",
        )(z, fin)
        return log_norm.reshape(rows), entropy.reshape(rows), target_logp.reshape(rows), log_probs

    return jax.shard_map(
        device_step,
        mesh=mesh,
        in_specs=(P("dp", None), P(None, "tp"), P(None, "tp"), P("tp", None), P(None),
                  P(None, "tp"), P("dp"), P("dp")),
        out_specs=(P("dp"), P("dp"), P("dp"), P("dp", None)),
        check_vma=False,
    )
```

time: 194 us -> 80.9 us (0.42)
  waiting for transfers between devices: 104 us -> 0 us
  Pallas kernels: 0 us -> 80.1 us
  matrix products: 35.7 us -> 0 us
  blocking collectives: 28 us -> 0 us
  between operations: 14.2 us -> 0.64 us
  local copies, waits for them, and re-layouts: 7.54 us -> 0 us
  other arithmetic: 4.75 us -> 0 us
    pallas_call x0 -> x2, Pallas kernels: none -> 80.1 us  [the longest x1 75.8 us: device_step(): pl.pallas_call(functools.partial(main_kernel, n), out_shape=(pltpu.VMEM((...]
    psum x1 -> x0, waiting for transfers between devices: 58.4 us -> none  [device_step(): mlp_out = lax.psum(part_sum, 'tp')]
    all_gather x1 -> x0, waiting for transfers between devices: 45.2 us -> none  [device_step(): log_probs = lax.all_gather(local_probs, 'tp', axis=1, tiled=True)]
    dot_general x3 -> x0, matrix products: 35.7 us -> none  [the longest x1 14.7 us: device_step(): jnp.dot(hidden_act, w_down, preferred_element_type=jnp.float32)]
    pmax x1 -> x0, blocking collectives: 14.6 us -> none  [device_step(): row_max = lax.pmax(jnp.max(logits, axis=-1), 'tp')]
    psum x1 -> x0, blocking collectives: 13.4 us -> none  [device_step(): row_stats = lax.psum(local_stats, 'tp')]
    unnamed x13 -> x0, local copies, waits for them, and re-layouts: 7.54 us -> none
    reduce_sum x2 -> x0, other arithmetic: 2.5 us -> none  [the longest x1 1.73 us: device_step(): jnp.mean(residual * residual, axis=-1, keepdims=True) + NORM_EPS]
  transfers between devices with their start and end apart: 2 -> 0, of which waited for: 2 -> 0; matrix products, arithmetic and copies ran while one was open for 0% -> 0% of each run, Pallas kernels for 0% -> 0%
where the time goes in v2:
time: 80.9 us; the launch traced here: 80.8 us
  Pallas kernels  80.1 us (99%)
    pallas_call x1, Pallas kernels, device_step(): pl.pallas_call(functools.partial(main_kernel, n), out_shape=(pltpu.VMEM((...  75.8 us
    pallas_call x1, Pallas kernels, device_step(): pl.pallas_call(finish_kernel, out_shape=(row, row, row, jax.ShapeDtypeStr...  4.32 us

profile of v2, /device:TPU:81, one launch (start us, length us, event | category | flops | bytes accessed | tf_op | source)
XLA Modules:
  0.0 80.8 jit_solution(10778682215696946242)
XLA Ops:
  0.6 75.8 %decode_tail.1 = (bf16[64,128,512]{2,1,0:T(8,128)(2,1)S(1)}, f32[8,128]{1,0:T(8,128)S(1)}) custom-call(bf16[128,4096]{1,0:T(8,128)(2,1)} %h_hbm.1, bf16[4096,1792]{1,0:T(8,128)(2,1)} %wg_hbm.1, bf16[4096,1792]{1,0:T(8,128)(2,1)} %wu_hbm.1, bf16[1792,4096]{1,0:T(8,128)(2,1)} %wd_hbm.1, f32[1,4096]{1,0:T(1,128)} %bitcast.6, bf16[4096,4096]{1,0:T(8,128)(2,1)} %wv_hbm.1, ...), custom_call_target="tpu_custom_call" | custom-call | tf_op jit(solution)/shard_map/decode_tail/pallas_call | solution.py:431
  76.5 4.3 %write_log_probs.1 = (f32[1,128]{1,0:T(1,128)}, f32[1,128]{1,0:T(1,128)}, f32[1,128]{1,0:T(1,128)}, bf16[128,32768]{1,0:T(8,128)(2,1)}) custom-call(bf16[64,128,512]{2,1,0:T(8,128)(2,1)S(1)} %get-tuple-element.10.z_ref, f32[8,128]{1,0:T(8,128)S(1)} %get-tuple-element.11.fin_ref), custom_call_target="tpu_custom_call" | custom-call | tf_op jit(solution)/shard_map/write_log_probs/pallas_call | solution.py:468

commit v3 on v2

v3 whole, which is shorter than its diff:
```python
import functools

import jax
import jax.numpy as jnp
from jax import lax
from jax.experimental import pallas as pl
from jax.experimental.pallas import tpu as pltpu
from jax.sharding import PartitionSpec as P

NORM_EPS = 1e-6
MESH = pl.DeviceIdType.MESH
F32 = jnp.float32
BF16 = jnp.bfloat16

SLAB = 256
AHEAD = 3
DOWN_AHEAD = 3
DOWN_SLOTS = 4
SPLIT = (1, 3)
GROUPS = len(SPLIT)
TILE = 512
EARLY = 3


class Ids:
    def __init__(self, chips, tiles):
        self.count = 0
        g = GROUPS
        self.part = self.take(chips)
        self.rs = self.take(3 * g)
        self.ynxt, self.yprv, self.yopp, self.ydie, self.fprv, self.fnxt, self.fopp = (self.take(g) for _ in range(7))
        self.znxt, self.zprv, self.zdie, self.zrel, self.zfp, self.zfn, self.zfo = (
            self.take(g * tiles) for _ in range(7))
        self.snxt, self.sprv, self.sopp, self.sdie, self.sfp, self.sfn, self.sfo = (self.take(1) for _ in range(7))

    def take(self, k):
        first = self.count
        self.count += k
        return first


def main_kernel(n, h_hbm, wg_hbm, wu_hbm, wd_hbm, gain_hbm, wv_hbm, temp_hbm, targ_hbm,
                z_ref, fin_ref,
                wbuf, dbuf, h_ref, a_ref, gu_ref, gain_ref, temp_ref, targ_ref,
                psend, prcv, rsend, rrcv, own_ref, ygat, cols_ref, st_ref, shift_ref, raw_ref,
                ss, rs, wsem, dsem, msem):
    chips = n // 2
    rows, dim = h_ref.shape
    unit = rows // sum(SPLIT)
    sizes = [unit * k for k in SPLIT]
    starts = [unit * sum(SPLIT[:g]) for g in range(GROUPS)]
    f_loc = a_ref.shape[1]
    nf = f_loc // SLAB
    own_w = dim // n
    tiles = z_ref.shape[0] // n
    per_tile = TILE // SLAB
    ids = Ids(chips, tiles)

    me = lax.axis_index("tp")
    chip, core = me // 2, me % 2
    other = 1 - core
    c_nxt, c_prv, c_opp = (chip + 1) % chips, (chip + chips - 1) % chips, (chip + 2) % chips
    nxt, prv, opp = c_nxt * 2 + core, c_prv * 2 + core, c_opp * 2 + core
    die = chip * 2 + other
    p_prv, p_nxt, p_opp = c_prv * 2 + other, c_nxt * 2 + other, c_opp * 2 + other

    def remote(src, dst, k, dev):
        return pltpu.make_async_remote_copy(src_ref=src, dst_ref=dst, send_sem=ss.at[k], recv_sem=rs.at[k],
                                            device_id={"tp": dev}, device_id_type=MESH)

    copies = []

    def send(ref, k, dev):
        c = remote(ref, ref, k, dev)
        c.start()
        copies.append(c)
        return c

    def arrived(ref, k):
        remote(ref, ref, k, die).wait_recv()

    def g_rows(g):
        return pl.ds(starts[g], sizes[g])

    def g_slice(g):
        return slice(starts[g], starts[g] + sizes[g])

    small = [pltpu.make_async_copy(h_hbm, h_ref, msem.at[0]),
             pltpu.make_async_copy(gain_hbm, gain_ref, msem.at[1]),
             pltpu.make_async_copy(temp_hbm, temp_ref, msem.at[2]),
             pltpu.make_async_copy(targ_hbm, targ_ref, msem.at[3])]

    def gate_up(j):
        col = pl.ds(pl.multiple_of(j * SLAB, SLAB), SLAB)
        return (pltpu.make_async_copy(wg_hbm.at[:, col], wbuf.at[2 * j], wsem.at[0, j]),
                pltpu.make_async_copy(wu_hbm.at[:, col], wbuf.at[2 * j + 1], wsem.at[1, j]))

    def start_gate_up(j):
        for c in gate_up(j):
            c.start()

    def vocab(s):
        col = pl.ds(pl.multiple_of(s * SLAB, SLAB), SLAB)
        return pltpu.make_async_copy(wv_hbm.at[:, col], wbuf.at[s], wsem.at[2, s])

    def down(k, dev):
        col = pl.ds(pl.multiple_of(dev * own_w, own_w), own_w)
        return pltpu.make_async_copy(wd_hbm.at[:, col], dbuf.at[k % DOWN_SLOTS], dsem.at[k])

    plan = ((c_opp, 0, True), (c_nxt, 1, True), (c_opp, 0, False), (c_prv, 2, True),
            (c_nxt, 1, False), (chip, 3, True), (c_prv, 2, False), (chip, 3, False))
    order = [c * 2 + (other if away else core) for c, _, away in plan]

    small[0].start()
    for j in range(AHEAD):
        start_gate_up(j)
    for c in small[1:]:
        c.start()

    barrier = pltpu.get_barrier_semaphore()
    for r in range(1, n):
        pl.semaphore_signal(barrier, inc=1, device_id={"tp": (me + r) % n}, device_id_type=MESH)

    small[0].wait()
    gu_ref[...] = jnp.zeros_like(gu_ref)

    def activate(j):
        act = jax.nn.silu(gu_ref[0]) * gu_ref[1]
        a_ref[:, pl.ds(pl.multiple_of(j * SLAB, SLAB), SLAB)] = act.astype(BF16)

    @pl.loop(0, nf)
    def _(j):
        for c in gate_up(j):
            c.wait()

        @pl.when(j + AHEAD < nf)
        def _():
            start_gate_up(j + AHEAD)

        for k in range(DOWN_AHEAD):
            @pl.when(j == nf - AHEAD + min(k, AHEAD - 1))
            def _():
                down(k, order[k]).start()

        activate(jnp.maximum(j - 1, 0))
        gate = jnp.dot(h_ref[...], wbuf[2 * j], preferred_element_type=F32)
        up = jnp.dot(h_ref[...], wbuf[2 * j + 1], preferred_element_type=F32)
        gu_ref[0] = gate
        gu_ref[1] = up

    activate(nf - 1)

    n_down = len(plan)
    owners = (opp, nxt, prv)

    def reduce_send(q, g):
        c = remote(rsend.at[q, g_rows(g)], rrcv.at[q, g_rows(g)], ids.rs + q * GROUPS + g, owners[q])
        c.start()
        copies.append(c)

    for k, (_, q, away) in enumerate(plan):
        if k + DOWN_AHEAD < n_down:
            down(k + DOWN_AHEAD, order[k + DOWN_AHEAD]).start()
        else:
            per = (tiles * per_tile) // DOWN_AHEAD
            first = (k + DOWN_AHEAD - n_down) * per
            last = tiles * per_tile if k == n_down - 1 else first + per
            for s in range(first, last):
                vocab(s).start()
        down(k, order[k]).wait()
        part = jnp.dot(a_ref[...], dbuf[k % DOWN_SLOTS], preferred_element_type=F32)
        to_die = remote(psend.at[q], prcv.at[q], ids.part + q, die)
        if k == 0:
            pl.semaphore_wait(barrier, n - 1)
        if away:
            psend[q] = part.astype(BF16)
            to_die.start()
            copies.append(to_die)
            continue
        to_die.wait_recv()
        total = part + prcv[q].astype(F32)
        if q < 3:
            rsend[q] = total.astype(BF16)
            reduce_send(q, 0)
        else:
            own_ref[...] = total

    for c in small[1:]:
        c.wait()
    row_ids = lax.broadcasted_iota(jnp.int32, (rows, rows), 0)
    lane_ids = lax.broadcasted_iota(jnp.int32, (rows, rows), 1)
    eye = row_ids == lane_ids
    inv_temp = 1.0 / jnp.sum(jnp.where(eye, temp_ref[...], 0.0), axis=1, keepdims=True)
    targ = jnp.sum(jnp.where(eye, targ_ref[...].astype(F32), 0.0), axis=1, keepdims=True)
    cols_ref[0] = jnp.broadcast_to(inv_temp, (rows, 128))
    cols_ref[1] = jnp.broadcast_to(targ, (rows, 128))
    cols_ref[2] = jnp.zeros((rows, 128), F32)

    def sum_and_send(g):
        sl = g_slice(g)
        for q in range(3):
            arrived(rrcv.at[q, g_rows(g)], ids.rs + q * GROUPS + g)
        y = own_ref[sl] + rrcv[0, sl].astype(F32) + rrcv[1, sl].astype(F32) + rrcv[2, sl].astype(F32)
        ygat[me, sl] = y.astype(BF16)
        own = ygat.at[me, g_rows(g)]
        send(own, ids.yopp + g, opp)
        send(own, ids.ynxt + g, nxt)
        send(own, ids.yprv + g, prv)
        send(own, ids.ydie + g, die)

    def residual(s, g):
        col = pl.ds(pl.multiple_of(s * own_w, own_w), own_w)
        return col, h_ref[g_rows(g), col].astype(F32) + ygat[s, g_slice(g)].astype(F32)

    def squares(s, g):
        _, r = residual(s, g)
        return jnp.sum(r * r, axis=1, keepdims=True)

    def finish_sum(g):
        for s, k, f in ((prv, ids.ynxt, ids.fprv), (nxt, ids.yprv, ids.fnxt), (opp, ids.yopp, ids.fopp)):
            arrived(ygat.at[s, g_rows(g)], k + g)
            send(ygat.at[s, g_rows(g)], f + g, die)

    def normalize(g):
        total_sq = squares(me, g) + squares(prv, g) + squares(nxt, g) + squares(opp, g)
        for s, k in ((die, ids.ydie), (p_prv, ids.fprv), (p_nxt, ids.fnxt), (p_opp, ids.fopp)):
            arrived(ygat.at[s, g_rows(g)], k + g)
            total_sq += squares(s, g)
        inv_rms = lax.rsqrt(total_sq * (1.0 / dim) + NORM_EPS)

        @pl.loop(0, n)
        def _(s):
            col, r = residual(s, g)
            h_ref[g_rows(g), col] = (gain_ref[:, col] * r * inv_rms).astype(BF16)


    def blk(dev, t, g):
        return raw_ref.at[dev * tiles + t, g_rows(g)]

    def own_sends(t, g):
        b = blk(me, t, g)
        at = g * tiles + t
        return (remote(b, b, ids.znxt + at, nxt), remote(b, b, ids.zprv + at, prv), remote(b, b, ids.zdie + at, die))

    def head(g, t0, t1):
        sl = g_slice(g)
        lanes = lax.broadcasted_iota(jnp.int32, (sizes[g], 128), 1)

        @pl.loop(t0, t1)
        def _(t):
            if g == 0:
                for i in range(per_tile):
                    vocab(t * per_tile + i).wait()
            pieces = [jnp.dot(h_ref[sl], wbuf[t * per_tile + i], preferred_element_type=F32) for i in range(per_tile)]
            logits = jnp.concatenate(pieces, axis=1) * cols_ref[0, sl][:, :1]
            top_l = jnp.max(logits, axis=1, keepdims=True)
            low = logits - top_l
            raw_ref[me * tiles + t, sl] = low.astype(BF16)
            for c in own_sends(t, g):
                c.start()
            e = jnp.exp(low)
            col_ids = lax.broadcasted_iota(jnp.int32, (sizes[g], TILE), 1) + (me * tiles + t) * TILE
            hit = jnp.where(col_ids.astype(F32) == cols_ref[1, sl][:, :1], logits, 0.0)
            stats = cols_ref[2, sl]
            for i, col in enumerate((top_l, jnp.sum(e, axis=1, keepdims=True),
                                     jnp.sum(e * logits, axis=1, keepdims=True), jnp.sum(hit, axis=1, keepdims=True))):
                stats = jnp.where(lanes == i * tiles + t, col, stats)
            cols_ref[2, sl] = stats

    sum_and_send(0)
    for g in range(1, GROUPS):
        for q in range(3):
            reduce_send(q, g)
    finish_sum(0)
    normalize(0)
    for g in range(GROUPS):
        head(g, 0, EARLY)
        if g + 1 < GROUPS:
            sum_and_send(g + 1)
        head(g, EARLY, tiles)
        if g + 1 < GROUPS:
            finish_sum(g + 1)
            normalize(g + 1)

    by_row = cols_ref[2].T
    tops = by_row[:tiles]
    scale = jnp.exp(tops - jnp.max(tops, axis=0, keepdims=True))
    st_ref[me] = jnp.concatenate(
        [tops, jnp.sum(by_row[tiles:2 * tiles] * scale, axis=0, keepdims=True),
         jnp.sum(by_row[2 * tiles:3 * tiles] * scale, axis=0, keepdims=True),
         jnp.sum(by_row[3 * tiles:4 * tiles], axis=0, keepdims=True),
         jnp.zeros((st_ref.shape[1] - tiles - 3, rows), F32)], axis=0)
    send(st_ref.at[me], ids.snxt, nxt)
    send(st_ref.at[me], ids.sprv, prv)
    send(st_ref.at[me], ids.sopp, opp)
    send(st_ref.at[me], ids.sdie, die)

    for g in range(GROUPS):
        for t in range(tiles):
            at = g * tiles + t
            copies += own_sends(t, g)
            arrived(blk(prv, t, g), ids.znxt + at)
            if t % 2 == 0:
                send(blk(prv, t, g), ids.zrel + at, nxt)
            send(blk(prv, t, g), ids.zfp + at, die)
            arrived(blk(nxt, t, g), ids.zprv + at)
            if t % 2 == 1:
                send(blk(nxt, t, g), ids.zrel + at, prv)
            send(blk(nxt, t, g), ids.zfn + at, die)

    arrived(st_ref.at[prv], ids.snxt)
    send(st_ref.at[prv], ids.sfp, die)
    arrived(st_ref.at[nxt], ids.sprv)
    send(st_ref.at[nxt], ids.sfn, die)
    arrived(st_ref.at[opp], ids.sopp)
    send(st_ref.at[opp], ids.sfo, die)
    for s, k in ((die, ids.sdie), (p_prv, ids.sfp), (p_nxt, ids.sfn), (p_opp, ids.sfo)):
        arrived(st_ref.at[s], k)

    dev_top = jnp.max(st_ref[:, :tiles], axis=1)
    top = jnp.max(dev_top, axis=0, keepdims=True)
    scale = jnp.exp(dev_top - top)
    sum_exp = jnp.sum(st_ref[:, tiles] * scale, axis=0, keepdims=True)
    weighted = jnp.sum(st_ref[:, tiles + 1] * scale, axis=0, keepdims=True)
    target_logit = jnp.sum(st_ref[:, tiles + 2], axis=0, keepdims=True)
    log_norm = top + jnp.log(sum_exp)
    fin_ref[0:1] = log_norm
    fin_ref[1:2] = log_norm - weighted / sum_exp
    fin_ref[2:3] = target_logit - log_norm
    pad = jnp.zeros((128 - tiles, rows), F32)

    for dev in range(n):
        shift_ref[dev] = jnp.concatenate([st_ref[dev, :tiles] - log_norm, pad], axis=0).T

    ready = []
    for t in range(tiles):
        ready += [("me", me, t), ("prv", prv, t), ("nxt", nxt, t), ("die", die, t), ("p_prv", p_prv, t), ("p_nxt", p_nxt, t)]
    landed = {"die": ids.zdie, "p_prv": ids.zfp, "p_nxt": ids.zfn, "p_opp": ids.zfo}

    def settle(items):
        for name, dev, t in items:
            if name in landed:
                for g in range(GROUPS):
                    arrived(blk(dev, t, g), landed[name] + g * tiles + t)
        for _, dev, t in items:
            b = dev * tiles + t
            z_ref[b] = (raw_ref[b].astype(F32) + shift_ref[dev][:, t:t + 1]).astype(BF16)

    steps = GROUPS * tiles
    taken = 0
    for g in range(GROUPS):
        for t in range(tiles):
            at = g * tiles + t
            upto = max(taken, (at * len(ready)) // (steps - 1))
            batch = ready[taken:upto]
            taken = upto
            if g == GROUPS - 1 and t > 1:
                batch += [("opp", opp, t - 2), ("p_opp", p_opp, t - 2)]
            settle(batch)
            arrived(blk(opp, t, g), ids.zrel + at)
            send(blk(opp, t, g), ids.zfo + at, die)
    settle([("opp", opp, tiles - 2), ("opp", opp, tiles - 1), ("p_opp", p_opp, tiles - 2)])
    settle([("p_opp", p_opp, tiles - 1)])
    for c in copies:
        c.wait_send()


def finish_kernel(z_ref, fin_ref, norm_hbm, ent_hbm, logp_hbm, out_hbm, sem):
    blocks, rows, width = z_ref.shape

    def put(b):
        return pltpu.make_async_copy(
            z_ref.at[b], out_hbm.at[:, pl.ds(pl.multiple_of(b * width, width), width)], sem.at[b])

    @pl.loop(0, blocks)
    def _(b):
        put(b).start()

    small = [pltpu.make_async_copy(fin_ref.at[pl.ds(i, 1)], ref, sem.at[blocks + i])
             for i, ref in enumerate((norm_hbm, ent_hbm, logp_hbm))]
    for c in small:
        c.start()

    @pl.loop(0, blocks)
    def _(b):
        put(b).wait()

    for c in small:
        c.wait()


def solution(mesh):
    n = mesh.shape["tp"]

    def device_step(hidden, w_gate, w_up, w_down, norm_gain, w_vocab, temperature, target):
        rows, dim = hidden.shape
        f_loc = w_gate.shape[1]
        v_loc = w_vocab.shape[1]
        own_w = dim // n
        tiles = v_loc // TILE
        n_ids = Ids(n // 2, tiles).count
        any_spec = pl.BlockSpec(memory_space=pl.ANY)
        vmem = pl.BlockSpec(memory_space=pltpu.VMEM)
        z, fin = pl.pallas_call(
            functools.partial(main_kernel, n),
            out_shape=(pltpu.VMEM((n * tiles, rows, TILE), BF16), pltpu.VMEM((8, rows), F32)),
            in_specs=[any_spec] * 8,
            out_specs=(vmem, vmem),
            scratch_shapes=[
                pltpu.VMEM((v_loc // SLAB, dim, SLAB), BF16),
                pltpu.VMEM((DOWN_SLOTS, f_loc, own_w), BF16),
                pltpu.VMEM((rows, dim), BF16),
                pltpu.VMEM((rows, f_loc), BF16),
                pltpu.VMEM((2, rows, SLAB), F32),
                pltpu.VMEM((1, dim), F32),
                pltpu.VMEM((1, rows), F32),
                pltpu.VMEM((1, rows), jnp.int32),
                pltpu.VMEM((4, rows, own_w), BF16),
                pltpu.VMEM((4, rows, own_w), BF16),
                pltpu.VMEM((3, rows, own_w), BF16),
                pltpu.VMEM((3, rows, own_w), BF16),
                pltpu.VMEM((rows, own_w), F32),
                pltpu.VMEM((n, rows, own_w), BF16),
                pltpu.VMEM((3, rows, 128), F32),
                pltpu.VMEM((n, 16, rows), F32),
                pltpu.VMEM((n, rows, 128), F32),
                pltpu.VMEM((n * tiles, rows, TILE), BF16),
                pltpu.SemaphoreType.DMA((n_ids,)),
                pltpu.SemaphoreType.DMA((n_ids,)),
                pltpu.SemaphoreType.DMA((3, v_loc // SLAB)),
                pltpu.SemaphoreType.DMA((n,)),
                pltpu.SemaphoreType.DMA((4,)),
            ],
            compiler_params=pltpu.CompilerParams(
                collective_id=0, has_side_effects=True, vmem_limit_bytes=57100 * 1024),
            name="decode_tail",
        )(hidden, w_gate, w_up, w_down, norm_gain.reshape(1, dim), w_vocab, temperature.reshape(1, rows),
          target.reshape(1, rows))
        row = jax.ShapeDtypeStruct((1, rows), F32)
        log_norm, entropy, target_logp, log_probs = pl.pallas_call(
            finish_kernel,
            out_shape=(row, row, row, jax.ShapeDtypeStruct((rows, n * v_loc), BF16)),
            in_specs=[vmem, vmem],
            out_specs=(any_spec,) * 4,
            scratch_shapes=[pltpu.SemaphoreType.DMA((n * tiles + 3,))],
            compiler_params=pltpu.CompilerParams(vmem_limit_bytes=4 * 1024 * 1024),
            name="write_log_probs",
        )(z, fin)
        return log_norm.reshape(rows), entropy.reshape(rows), target_logp.reshape(rows), log_probs

    return jax.shard_map(
        device_step,
        mesh=mesh,
        in_specs=(P("dp", None), P(None, "tp"), P(None, "tp"), P("tp", None), P(None),
                  P(None, "tp"), P("dp"), P("dp")),
        out_specs=(P("dp"), P("dp"), P("dp"), P("dp", None)),
        check_vma=False,
    )
```

time: 80.9 us -> 79.8 us (0.986)
  Pallas kernels: 80.1 us -> 79.1 us
where the time goes in v3:
time: 79.8 us
  Pallas kernels  79.1 us (99%)
    pallas_call x1, Pallas kernels, device_step(): pl.pallas_call(functools.partial(main_kernel, n), out_shape=(pltpu.VMEM((...  75.3 us
    pallas_call x1, Pallas kernels, device_step(): pl.pallas_call(finish_kernel, out_shape=(row, row, row, jax.ShapeDtypeStr...  3.83 us

profile of v3, /device:TPU:81, one launch (start us, length us, event | category | flops | bytes accessed | tf_op | source)
XLA Modules:
  0.0 79.8 jit_solution(11388458447587305746)
XLA Ops:
  0.6 75.3 %decode_tail.1 = (bf16[64,128,512]{2,1,0:T(8,128)(2,1)S(1)}, f32[8,128]{1,0:T(8,128)S(1)}) custom-call(bf16[128,4096]{1,0:T(8,128)(2,1)} %h_hbm.1, bf16[4096,1792]{1,0:T(8,128)(2,1)} %wg_hbm.1, bf16[4096,1792]{1,0:T(8,128)(2,1)} %wu_hbm.1, bf16[1792,4096]{1,0:T(8,128)(2,1)} %wd_hbm.1, f32[1,4096]{1,0:T(1,128)} %bitcast.6, bf16[4096,4096]{1,0:T(8,128)(2,1)} %wv_hbm.1, ...), custom_call_target="tpu_custom_call" | custom-call | tf_op jit(solution)/shard_map/decode_tail/pallas_call | solution.py:404
  75.9 3.8 %write_log_probs.1 = (f32[1,128]{1,0:T(1,128)}, f32[1,128]{1,0:T(1,128)}, f32[1,128]{1,0:T(1,128)}, bf16[128,32768]{1,0:T(8,128)(2,1)}) custom-call(bf16[64,128,512]{2,1,0:T(8,128)(2,1)S(1)} %get-tuple-element.10.z_ref, f32[8,128]{1,0:T(8,128)S(1)} %get-tuple-element.11.fin_ref), custom_call_target="tpu_custom_call" | custom-call | tf_op jit(solution)/shard_map/write_log_probs/pallas_call | solution.py:440

commit v4 on v3

--- a/solution.py
+++ b/solution.py
@@ -16,10 +16,11 @@
 AHEAD = 3
 DOWN_AHEAD = 3
 DOWN_SLOTS = 4
-SPLIT = (1, 3)
+SPLIT = (3, 5)
 GROUPS = len(SPLIT)
+RELAYED = 6
 TILE = 512
-EARLY = 3
+EARLY = 6
 
 
 class Ids:
@@ -95,9 +96,22 @@
         return (pltpu.make_async_copy(wg_hbm.at[:, col], wbuf.at[2 * j], wsem.at[0, j]),
                 pltpu.make_async_copy(wu_hbm.at[:, col], wbuf.at[2 * j + 1], wsem.at[1, j]))
 
+    def last_pair(part):
+        rws = pl.ds(part * (dim // 2), dim // 2)
+        col = pl.ds((nf - 1) * SLAB, SLAB)
+        return (pltpu.make_async_copy(wg_hbm.at[rws, col], wbuf.at[2 * nf - 2, rws], wsem.at[0, nf - 1 + part]),
+                pltpu.make_async_copy(wu_hbm.at[rws, col], wbuf.at[2 * nf - 1, rws], wsem.at[1, nf - 1 + part]))
+
     def start_gate_up(j):
-        for c in gate_up(j):
-            c.start()
+        @pl.when(j < nf - 1)
+        def _():
+            for c in gate_up(j):
+                c.start()
+
+        @pl.when(j == nf - 1)
+        def _():
+            for c in last_pair(0) + last_pair(1):
+                c.start()
 
     def vocab(s):
         col = pl.ds(pl.multiple_of(s * SLAB, SLAB), SLAB)
@@ -107,8 +121,8 @@
         col = pl.ds(pl.multiple_of(dev * own_w, own_w), own_w)
         return pltpu.make_async_copy(wd_hbm.at[:, col], dbuf.at[k % DOWN_SLOTS], dsem.at[k])
 
-    plan = ((c_opp, 0, True), (c_nxt, 1, True), (c_opp, 0, False), (c_prv, 2, True),
-            (c_nxt, 1, False), (chip, 3, True), (c_prv, 2, False), (chip, 3, False))
+    plan = ((c_opp, 0, True), (c_nxt, 1, True), (c_prv, 2, True), (c_opp, 0, False),
+            (c_nxt, 1, False), (c_prv, 2, False), (chip, 3, True), (chip, 3, False))
     order = [c * 2 + (other if away else core) for c, _, away in plan]
 
     small[0].start()
@@ -128,7 +142,7 @@
         act = jax.nn.silu(gu_ref[0]) * gu_ref[1]
         a_ref[:, pl.ds(pl.multiple_of(j * SLAB, SLAB), SLAB)] = act.astype(BF16)
 
-    @pl.loop(0, nf)
+    @pl.loop(0, nf - 1)
     def _(j):
         for c in gate_up(j):
             c.wait()
@@ -138,7 +152,7 @@
             start_gate_up(j + AHEAD)
 
         for k in range(DOWN_AHEAD):
-            @pl.when(j == nf - AHEAD + min(k, AHEAD - 1))
+            @pl.when(j == nf - AHEAD + min(k, AHEAD - 2))
             def _():
                 down(k, order[k]).start()
 
@@ -148,6 +162,16 @@
         gu_ref[0] = gate
         gu_ref[1] = up
 
+    for c in last_pair(0):
+        c.wait()
+    kh = dim // 2
+    activate(nf - 2)
+    gu_ref[0] = jnp.dot(h_ref[:, :kh], wbuf[2 * nf - 2, :kh], preferred_element_type=F32)
+    gu_ref[1] = jnp.dot(h_ref[:, :kh], wbuf[2 * nf - 1, :kh], preferred_element_type=F32)
+    for c in last_pair(1):
+        c.wait()
+    gu_ref[0] += jnp.dot(h_ref[:, kh:], wbuf[2 * nf - 2, kh:], preferred_element_type=F32)
+    gu_ref[1] += jnp.dot(h_ref[:, kh:], wbuf[2 * nf - 1, kh:], preferred_element_type=F32)
     activate(nf - 1)
 
     n_down = len(plan)
@@ -182,6 +206,10 @@
         if q < 3:
             rsend[q] = total.astype(BF16)
             reduce_send(q, 0)
+            if q == 2:
+                for g in range(1, GROUPS):
+                    for r in range(3):
+                        reduce_send(r, g)
         else:
             own_ref[...] = total
 
@@ -267,19 +295,30 @@
                 stats = jnp.where(lanes == i * tiles + t, col, stats)
             cols_ref[2, sl] = stats
 
-    sum_and_send(0)
-    for g in range(1, GROUPS):
-        for q in range(3):
-            reduce_send(q, g)
+    def near(g, t0, t1):
+        for t in range(t0, t1):
+            at = g * tiles + t
+            copies.extend(own_sends(t, g))
+            arrived(blk(prv, t, g), ids.znxt + at)
+            if t % 2 == 0:
+                send(blk(prv, t, g), ids.zrel + at, nxt)
+            send(blk(prv, t, g), ids.zfp + at, die)
+            arrived(blk(nxt, t, g), ids.zprv + at)
+            if t % 2 == 1:
+                send(blk(nxt, t, g), ids.zrel + at, prv)
+            send(blk(nxt, t, g), ids.zfn + at, die)
+
+    for g in range(GROUPS):
+        sum_and_send(g)
     finish_sum(0)
     normalize(0)
     for g in range(GROUPS):
         head(g, 0, EARLY)
         if g + 1 < GROUPS:
-            sum_and_send(g + 1)
+            finish_sum(g + 1)
         head(g, EARLY, tiles)
         if g + 1 < GROUPS:
-            finish_sum(g + 1)
+            near(g, 0, RELAYED)
             normalize(g + 1)
 
     by_row = cols_ref[2].T
@@ -296,17 +335,7 @@
     send(st_ref.at[me], ids.sdie, die)
 
     for g in range(GROUPS):
-        for t in range(tiles):
-            at = g * tiles + t
-            copies += own_sends(t, g)
-            arrived(blk(prv, t, g), ids.znxt + at)
-            if t % 2 == 0:
-                send(blk(prv, t, g), ids.zrel + at, nxt)
-            send(blk(prv, t, g), ids.zfp + at, die)
-            arrived(blk(nxt, t, g), ids.zprv + at)
-            if t % 2 == 1:
-                send(blk(nxt, t, g), ids.zrel + at, prv)
-            send(blk(nxt, t, g), ids.zfn + at, die)
+        near(g, RELAYED if g + 1 < GROUPS else 0, tiles)
 
     arrived(st_ref.at[prv], ids.snxt)
     send(st_ref.at[prv], ids.sfp, die)

time: 79.8 us -> 74.7 us (0.936)
  Pallas kernels: 79.1 us -> 73.8 us
    pallas_call x1, Pallas kernels: 75.3 us -> 70 us  [device_step(): pl.pallas_call(functools.partial(main_kernel, n), out_shape=(pltpu.VMEM((...]
where the time goes in v4:
time: 74.7 us; the launch traced here: 74.6 us
  Pallas kernels  73.8 us (99%)
  between operations  0.8 us (1%)
    pallas_call x1, Pallas kernels, device_step(): pl.pallas_call(functools.partial(main_kernel, n), out_shape=(pltpu.VMEM((...  70 us
    pallas_call x1, Pallas kernels, device_step(): pl.pallas_call(finish_kernel, out_shape=(row, row, row, jax.ShapeDtypeStr...  3.83 us

profile of v4, /device:TPU:81, one launch (start us, length us, event | category | flops | bytes accessed | tf_op | source)
XLA Modules:
  0.0 74.6 jit_solution(7605228016971302625)
XLA Ops:
  0.6 70.0 %decode_tail.1 = (bf16[64,128,512]{2,1,0:T(8,128)(2,1)S(1)}, f32[8,128]{1,0:T(8,128)S(1)}) custom-call(bf16[128,4096]{1,0:T(8,128)(2,1)} %h_hbm.1, bf16[4096,1792]{1,0:T(8,128)(2,1)} %wg_hbm.1, bf16[4096,1792]{1,0:T(8,128)(2,1)} %wu_hbm.1, bf16[1792,4096]{1,0:T(8,128)(2,1)} %wd_hbm.1, f32[1,4096]{1,0:T(1,128)} %bitcast.6, bf16[4096,4096]{1,0:T(8,128)(2,1)} %wv_hbm.1, ...), custom_call_target="tpu_custom_call" | custom-call | tf_op jit(solution)/shard_map/decode_tail/pallas_call | solution.py:433
  70.6 3.8 %write_log_probs.1 = (f32[1,128]{1,0:T(1,128)}, f32[1,128]{1,0:T(1,128)}, f32[1,128]{1,0:T(1,128)}, bf16[128,32768]{1,0:T(8,128)(2,1)}) custom-call(bf16[64,128,512]{2,1,0:T(8,128)(2,1)S(1)} %get-tuple-element.10.z_ref, f32[8,128]{1,0:T(8,128)S(1)} %get-tuple-element.11.fin_ref), custom_call_target="tpu_custom_call" | custom-call | tf_op jit(solution)/shard_map/write_log_probs/pallas_call | solution.py:469

commit v5 on v4

--- a/solution.py
+++ b/solution.py
@@ -20,7 +20,10 @@
 GROUPS = len(SPLIT)
 RELAYED = 6
 TILE = 512
-EARLY = 6
+FIRST, EARLY = 2, 6
+
+
+SEND_Y, SEND_Z, SEND_STATS = range(3)
 
 
 class Ids:
@@ -28,10 +31,11 @@
         self.count = 0
         g = GROUPS
         self.part = self.take(chips)
-        self.rs = self.take(3 * g)
+        self.rs = self.take(g)
         self.ynxt, self.yprv, self.yopp, self.ydie, self.fprv, self.fnxt, self.fopp = (self.take(g) for _ in range(7))
-        self.znxt, self.zprv, self.zdie, self.zrel, self.zfp, self.zfn, self.zfo = (
-            self.take(g * tiles) for _ in range(7))
+        self.ytop, self.ybot, self.ftop, self.fbot = (self.take(g - 1) for _ in range(4))
+        self.znxt, self.zprv, self.zrel = (self.take(g * tiles) for _ in range(3))
+        self.zdie, self.zfar = self.take(tiles), self.take(tiles)
         self.snxt, self.sprv, self.sopp, self.sdie, self.sfp, self.sfn, self.sfo = (self.take(1) for _ in range(7))
 
     def take(self, k):
@@ -44,7 +48,7 @@
                 z_ref, fin_ref,
                 wbuf, dbuf, h_ref, a_ref, gu_ref, gain_ref, temp_ref, targ_ref,
                 psend, prcv, rsend, rrcv, own_ref, ygat, cols_ref, st_ref, shift_ref, raw_ref,
-                ss, rs, wsem, dsem, msem):
+                ss, rs, wsem, vsem, dsem, msem):
     chips = n // 2
     rows, dim = h_ref.shape
     unit = rows // sum(SPLIT)
@@ -65,20 +69,18 @@
     die = chip * 2 + other
     p_prv, p_nxt, p_opp = c_prv * 2 + other, c_nxt * 2 + other, c_opp * 2 + other
 
-    def remote(src, dst, k, dev):
-        return pltpu.make_async_remote_copy(src_ref=src, dst_ref=dst, send_sem=ss.at[k], recv_sem=rs.at[k],
+    def remote(src, dst, k, dev, kind):
+        return pltpu.make_async_remote_copy(src_ref=src, dst_ref=dst, send_sem=ss.at[kind], recv_sem=rs.at[k],
                                             device_id={"tp": dev}, device_id_type=MESH)
 
-    copies = []
-
-    def send(ref, k, dev):
-        c = remote(ref, ref, k, dev)
-        c.start()
-        copies.append(c)
-        return c
+    def send(ref, k, dev, kind=SEND_Y):
+        remote(ref, ref, k, dev, kind).start()
 
     def arrived(ref, k):
-        remote(ref, ref, k, die).wait_recv()
+        remote(ref, ref, k, die, SEND_Y).wait_recv()
+
+    def landed(ref, sem):
+        pltpu.make_async_copy(ref, ref, sem).wait()
 
     def g_rows(g):
         return pl.ds(starts[g], sizes[g])
@@ -93,14 +95,14 @@
 
     def gate_up(j):
         col = pl.ds(pl.multiple_of(j * SLAB, SLAB), SLAB)
-        return (pltpu.make_async_copy(wg_hbm.at[:, col], wbuf.at[2 * j], wsem.at[0, j]),
-                pltpu.make_async_copy(wu_hbm.at[:, col], wbuf.at[2 * j + 1], wsem.at[1, j]))
+        return (pltpu.make_async_copy(wg_hbm.at[:, col], wbuf.at[2 * j], wsem.at[j]),
+                pltpu.make_async_copy(wu_hbm.at[:, col], wbuf.at[2 * j + 1], wsem.at[j]))
 
     def last_pair(part):
         rws = pl.ds(part * (dim // 2), dim // 2)
         col = pl.ds((nf - 1) * SLAB, SLAB)
-        return (pltpu.make_async_copy(wg_hbm.at[rws, col], wbuf.at[2 * nf - 2, rws], wsem.at[0, nf - 1 + part]),
-                pltpu.make_async_copy(wu_hbm.at[rws, col], wbuf.at[2 * nf - 1, rws], wsem.at[1, nf - 1 + part]))
+        return (pltpu.make_async_copy(wg_hbm.at[rws, col], wbuf.at[2 * nf - 2, rws], wsem.at[nf - 1 + part]),
+                pltpu.make_async_copy(wu_hbm.at[rws, col], wbuf.at[2 * nf - 1, rws], wsem.at[nf - 1 + part]))
 
     def start_gate_up(j):
         @pl.when(j < nf - 1)
@@ -115,7 +117,7 @@
 
     def vocab(s):
         col = pl.ds(pl.multiple_of(s * SLAB, SLAB), SLAB)
-        return pltpu.make_async_copy(wv_hbm.at[:, col], wbuf.at[s], wsem.at[2, s])
+        return pltpu.make_async_copy(wv_hbm.at[:, col], wbuf.at[s], vsem.at[s // per_tile])
 
     def down(k, dev):
         col = pl.ds(pl.multiple_of(dev * own_w, own_w), own_w)
@@ -144,8 +146,7 @@
 
     @pl.loop(0, nf - 1)
     def _(j):
-        for c in gate_up(j):
-            c.wait()
+        landed(wbuf.at[pl.ds(2 * j, 2)], wsem.at[j])
 
         @pl.when(j + AHEAD < nf)
         def _():
@@ -162,14 +163,12 @@
         gu_ref[0] = gate
         gu_ref[1] = up
 
-    for c in last_pair(0):
-        c.wait()
+    landed(wbuf.at[pl.ds(2 * nf - 2, 2), pl.ds(0 * (dim // 2), dim // 2)], wsem.at[nf - 1 + 0])
     kh = dim // 2
     activate(nf - 2)
     gu_ref[0] = jnp.dot(h_ref[:, :kh], wbuf[2 * nf - 2, :kh], preferred_element_type=F32)
     gu_ref[1] = jnp.dot(h_ref[:, :kh], wbuf[2 * nf - 1, :kh], preferred_element_type=F32)
-    for c in last_pair(1):
-        c.wait()
+    landed(wbuf.at[pl.ds(2 * nf - 2, 2), pl.ds(1 * (dim // 2), dim // 2)], wsem.at[nf - 1 + 1])
     gu_ref[0] += jnp.dot(h_ref[:, kh:], wbuf[2 * nf - 2, kh:], preferred_element_type=F32)
     gu_ref[1] += jnp.dot(h_ref[:, kh:], wbuf[2 * nf - 1, kh:], preferred_element_type=F32)
     activate(nf - 1)
@@ -178,9 +177,7 @@
     owners = (opp, nxt, prv)
 
     def reduce_send(q, g):
-        c = remote(rsend.at[q, g_rows(g)], rrcv.at[q, g_rows(g)], ids.rs + q * GROUPS + g, owners[q])
-        c.start()
-        copies.append(c)
+        remote(rsend.at[q, g_rows(g)], rrcv.at[q, g_rows(g)], ids.rs + g, owners[q], SEND_Y).start()
 
     for k, (_, q, away) in enumerate(plan):
         if k + DOWN_AHEAD < n_down:
@@ -193,25 +190,23 @@
                 vocab(s).start()
         down(k, order[k]).wait()
         part = jnp.dot(a_ref[...], dbuf[k % DOWN_SLOTS], preferred_element_type=F32)
-        to_die = remote(psend.at[q], prcv.at[q], ids.part + q, die)
+        to_die = remote(psend.at[q], prcv.at[q], ids.part + q, die, SEND_Y)
         if k == 0:
             pl.semaphore_wait(barrier, n - 1)
         if away:
             psend[q] = part.astype(BF16)
             to_die.start()
-            copies.append(to_die)
             continue
         to_die.wait_recv()
         total = part + prcv[q].astype(F32)
         if q < 3:
             rsend[q] = total.astype(BF16)
             reduce_send(q, 0)
-            if q == 2:
-                for g in range(1, GROUPS):
-                    for r in range(3):
-                        reduce_send(r, g)
         else:
             own_ref[...] = total
+    for g in range(1, GROUPS):
+        for q in range(3):
+            reduce_send(q, g)
 
     for c in small[1:]:
         c.wait()
@@ -226,12 +221,12 @@
 
     def sum_and_send(g):
         sl = g_slice(g)
-        for q in range(3):
-            arrived(rrcv.at[q, g_rows(g)], ids.rs + q * GROUPS + g)
+        arrived(rrcv.at[:, g_rows(g)], ids.rs + g)
         y = own_ref[sl] + rrcv[0, sl].astype(F32) + rrcv[1, sl].astype(F32) + rrcv[2, sl].astype(F32)
         ygat[me, sl] = y.astype(BF16)
         own = ygat.at[me, g_rows(g)]
-        send(own, ids.yopp + g, opp)
+        if g == 0:
+            send(own, ids.yopp + g, opp)
         send(own, ids.ynxt + g, nxt)
         send(own, ids.yprv + g, prv)
         send(own, ids.ydie + g, die)
@@ -244,16 +239,39 @@
         _, r = residual(s, g)
         return jnp.sum(r * r, axis=1, keepdims=True)
 
-    def finish_sum(g):
-        for s, k, f in ((prv, ids.ynxt, ids.fprv), (nxt, ids.yprv, ids.fnxt), (opp, ids.yopp, ids.fopp)):
+    def halves(g):
+        top = (sizes[g] // 2 + 15) // 16 * 16
+        return pl.ds(starts[g], top), pl.ds(starts[g] + top, sizes[g] - top)
+
+    def forward_near(g):
+        for s, k, f in ((prv, ids.ynxt, ids.fprv), (nxt, ids.yprv, ids.fnxt)):
             arrived(ygat.at[s, g_rows(g)], k + g)
+            if g > 0 and s is prv:
+                send(ygat.at[s, halves(g)[0]], ids.ytop + g - 1, nxt)
+            elif g > 0:
+                send(ygat.at[s, halves(g)[1]], ids.ybot + g - 1, prv)
             send(ygat.at[s, g_rows(g)], f + g, die)
+
+    def forward_far(g):
+        if g == 0:
+            arrived(ygat.at[opp, g_rows(g)], ids.yopp + g)
+            send(ygat.at[opp, g_rows(g)], ids.fopp + g, die)
+            return
+        for rws, k, f in zip(halves(g), (ids.ytop, ids.ybot), (ids.ftop, ids.fbot)):
+            arrived(ygat.at[opp, rws], k + g - 1)
+            send(ygat.at[opp, rws], f + g - 1, die)
 
     def normalize(g):
         total_sq = squares(me, g) + squares(prv, g) + squares(nxt, g) + squares(opp, g)
-        for s, k in ((die, ids.ydie), (p_prv, ids.fprv), (p_nxt, ids.fnxt), (p_opp, ids.fopp)):
+        for s, k in ((die, ids.ydie), (p_prv, ids.fprv), (p_nxt, ids.fnxt)):
             arrived(ygat.at[s, g_rows(g)], k + g)
             total_sq += squares(s, g)
+        if g == 0:
+            arrived(ygat.at[p_opp, g_rows(g)], ids.fopp + g)
+        else:
+            for rws, k in zip(halves(g), (ids.ftop, ids.fbot)):
+                arrived(ygat.at[p_opp, rws], k + g - 1)
+        total_sq += squares(p_opp, g)
         inv_rms = lax.rsqrt(total_sq * (1.0 / dim) + NORM_EPS)
 
         @pl.loop(0, n)
@@ -268,7 +286,8 @@
     def own_sends(t, g):
         b = blk(me, t, g)
         at = g * tiles + t
-        return (remote(b, b, ids.znxt + at, nxt), remote(b, b, ids.zprv + at, prv), remote(b, b, ids.zdie + at, die))
+        return (remote(b, b, ids.znxt + at, nxt, SEND_Z), remote(b, b, ids.zprv + at, prv, SEND_Z),
+                remote(b, b, ids.zdie + t, die, SEND_Z))
 
     def head(g, t0, t1):
         sl = g_slice(g)
@@ -277,8 +296,7 @@
         @pl.loop(t0, t1)
         def _(t):
             if g == 0:
-                for i in range(per_tile):
-                    vocab(t * per_tile + i).wait()
+                landed(wbuf.at[pl.ds(t * per_tile, per_tile)], vsem.at[t])
             pieces = [jnp.dot(h_ref[sl], wbuf[t * per_tile + i], preferred_element_type=F32) for i in range(per_tile)]
             logits = jnp.concatenate(pieces, axis=1) * cols_ref[0, sl][:, :1]
             top_l = jnp.max(logits, axis=1, keepdims=True)
@@ -298,26 +316,30 @@
     def near(g, t0, t1):
         for t in range(t0, t1):
             at = g * tiles + t
-            copies.extend(own_sends(t, g))
             arrived(blk(prv, t, g), ids.znxt + at)
             if t % 2 == 0:
-                send(blk(prv, t, g), ids.zrel + at, nxt)
-            send(blk(prv, t, g), ids.zfp + at, die)
+                send(blk(prv, t, g), ids.zrel + at, nxt, SEND_Z)
+            send(blk(prv, t, g), ids.zdie + t, die, SEND_Z)
             arrived(blk(nxt, t, g), ids.zprv + at)
             if t % 2 == 1:
-                send(blk(nxt, t, g), ids.zrel + at, prv)
-            send(blk(nxt, t, g), ids.zfn + at, die)
+                send(blk(nxt, t, g), ids.zrel + at, prv, SEND_Z)
+            send(blk(nxt, t, g), ids.zdie + t, die, SEND_Z)
 
     for g in range(GROUPS):
         sum_and_send(g)
-    finish_sum(0)
+    forward_near(0)
+    forward_far(0)
     normalize(0)
     for g in range(GROUPS):
-        head(g, 0, EARLY)
-        if g + 1 < GROUPS:
-            finish_sum(g + 1)
+        more = g + 1 < GROUPS
+        head(g, 0, FIRST)
+        if more:
+            forward_near(g + 1)
+        head(g, FIRST, EARLY)
+        if more:
+            forward_far(g + 1)
         head(g, EARLY, tiles)
-        if g + 1 < GROUPS:
+        if more:
             near(g, 0, RELAYED)
             normalize(g + 1)
 
@@ -329,20 +351,20 @@
          jnp.sum(by_row[2 * tiles:3 * tiles] * scale, axis=0, keepdims=True),
          jnp.sum(by_row[3 * tiles:4 * tiles], axis=0, keepdims=True),
          jnp.zeros((st_ref.shape[1] - tiles - 3, rows), F32)], axis=0)
-    send(st_ref.at[me], ids.snxt, nxt)
-    send(st_ref.at[me], ids.sprv, prv)
-    send(st_ref.at[me], ids.sopp, opp)
-    send(st_ref.at[me], ids.sdie, die)
+    send(st_ref.at[me], ids.snxt, nxt, SEND_STATS)
+    send(st_ref.at[me], ids.sprv, prv, SEND_STATS)
+    send(st_ref.at[me], ids.sopp, opp, SEND_STATS)
+    send(st_ref.at[me], ids.sdie, die, SEND_STATS)
 
     for g in range(GROUPS):
         near(g, RELAYED if g + 1 < GROUPS else 0, tiles)
 
     arrived(st_ref.at[prv], ids.snxt)
-    send(st_ref.at[prv], ids.sfp, die)
+    send(st_ref.at[prv], ids.sfp, die, SEND_STATS)
     arrived(st_ref.at[nxt], ids.sprv)
-    send(st_ref.at[nxt], ids.sfn, die)
+    send(st_ref.at[nxt], ids.sfn, die, SEND_STATS)
     arrived(st_ref.at[opp], ids.sopp)
-    send(st_ref.at[opp], ids.sfo, die)
+    send(st_ref.at[opp], ids.sfo, die, SEND_STATS)
     for s, k in ((die, ids.sdie), (p_prv, ids.sfp), (p_nxt, ids.sfn), (p_opp, ids.sfo)):
         arrived(st_ref.at[s], k)
 
@@ -363,14 +385,17 @@
 
     ready = []
     for t in range(tiles):
-        ready += [("me", me, t), ("prv", prv, t), ("nxt", nxt, t), ("die", die, t), ("p_prv", p_prv, t), ("p_nxt", p_nxt, t)]
-    landed = {"die": ids.zdie, "p_prv": ids.zfp, "p_nxt": ids.zfn, "p_opp": ids.zfo}
+        ready += [("own", me, t), ("near", prv, t), ("near", nxt, t), ("die", die, t), ("die", p_prv, t), ("die", p_nxt, t)]
+
+    seen = set()
 
     def settle(items):
         for name, dev, t in items:
-            if name in landed:
-                for g in range(GROUPS):
-                    arrived(blk(dev, t, g), landed[name] + g * tiles + t)
+            if name == "die" and ("die", t) not in seen:
+                arrived(raw_ref.at[pl.ds(0, 3)], ids.zdie + t)
+            if name == "far":
+                arrived(raw_ref.at[0], ids.zfar + t)
+            seen.add((name, t))
         for _, dev, t in items:
             b = dev * tiles + t
             z_ref[b] = (raw_ref[b].astype(F32) + shift_ref[dev][:, t:t + 1]).astype(BF16)
@@ -384,38 +409,29 @@
             batch = ready[taken:upto]
             taken = upto
             if g == GROUPS - 1 and t > 1:
-                batch += [("opp", opp, t - 2), ("p_opp", p_opp, t - 2)]
+                batch += [("opp", opp, t - 2), ("far", p_opp, t - 2)]
             settle(batch)
             arrived(blk(opp, t, g), ids.zrel + at)
-            send(blk(opp, t, g), ids.zfo + at, die)
-    settle([("opp", opp, tiles - 2), ("opp", opp, tiles - 1), ("p_opp", p_opp, tiles - 2)])
-    settle([("p_opp", p_opp, tiles - 1)])
-    for c in copies:
-        c.wait_send()
+            send(blk(opp, t, g), ids.zfar + t, die, SEND_Z)
+    settle([("opp", opp, tiles - 2), ("opp", opp, tiles - 1), ("far", p_opp, tiles - 2)])
+    settle([("far", p_opp, tiles - 1)])
+    for ref, kind in ((raw_ref.at[pl.ds(0, 2 * chips + 6)], SEND_Y), (raw_ref.at[pl.ds(0, 7 * tiles)], SEND_Z),
+                      (st_ref.at[pl.ds(0, 7)], SEND_STATS)):
+        remote(ref, ref, ids.part, die, kind).wait_send()
 
 
 def finish_kernel(z_ref, fin_ref, norm_hbm, ent_hbm, logp_hbm, out_hbm, sem):
     blocks, rows, width = z_ref.shape
 
-    def put(b):
-        return pltpu.make_async_copy(
-            z_ref.at[b], out_hbm.at[:, pl.ds(pl.multiple_of(b * width, width), width)], sem.at[b])
-
     @pl.loop(0, blocks)
     def _(b):
-        put(b).start()
-
-    small = [pltpu.make_async_copy(fin_ref.at[pl.ds(i, 1)], ref, sem.at[blocks + i])
-             for i, ref in enumerate((norm_hbm, ent_hbm, logp_hbm))]
-    for c in small:
-        c.start()
-
-    @pl.loop(0, blocks)
-    def _(b):
-        put(b).wait()
-
-    for c in small:
-        c.wait()
+        pltpu.make_async_copy(
+            z_ref.at[b], out_hbm.at[:, pl.ds(pl.multiple_of(b * width, width), width)], sem.at[0]).start()
+
+    for i, ref in enumerate((norm_hbm, ent_hbm, logp_hbm)):
+        pltpu.make_async_copy(fin_ref.at[pl.ds(i, 1)], ref, sem.at[1]).start()
+    pltpu.make_async_copy(z_ref, z_ref, sem.at[0]).wait()
+    pltpu.make_async_copy(fin_ref.at[pl.ds(0, 3)], fin_ref.at[pl.ds(0, 3)], sem.at[1]).wait()
 
 
 def solution(mesh):
@@ -454,9 +470,10 @@
                 pltpu.VMEM((n, 16, rows), F32),
                 pltpu.VMEM((n, rows, 128), F32),
                 pltpu.VMEM((n * tiles, rows, TILE), BF16),
+                pltpu.SemaphoreType.DMA((3,)),
                 pltpu.SemaphoreType.DMA((n_ids,)),
-                pltpu.SemaphoreType.DMA((n_ids,)),
-                pltpu.SemaphoreType.DMA((3, v_loc // SLAB)),
+                pltpu.SemaphoreType.DMA((f_loc // SLAB + 1,)),
+                pltpu.SemaphoreType.DMA((tiles,)),
                 pltpu.SemaphoreType.DMA((n,)),
                 pltpu.SemaphoreType.DMA((4,)),
             ],
@@ -471,7 +488,7 @@
             out_shape=(row, row, row, jax.ShapeDtypeStruct((rows, n * v_loc), BF16)),
             in_specs=[vmem, vmem],
             out_specs=(any_spec,) * 4,
-            scratch_shapes=[pltpu.SemaphoreType.DMA((n * tiles + 3,))],
+            scratch_shapes=[pltpu.SemaphoreType.DMA((2,))],
             compiler_params=pltpu.CompilerParams(vmem_limit_bytes=4 * 1024 * 1024),
             name="write_log_probs",
         )(z, fin)

time: 74.7 us -> 73.1 us (0.979)
  Pallas kernels: 73.8 us -> 72.2 us
    pallas_call x1, Pallas kernels: 70 us -> 69 us  [device_step(): pl.pallas_call(functools.partial(main_kernel, n), out_shape=(pltpu.VMEM((...]
where the time goes in v5:
time: 73.1 us; the launch traced here: 73 us
  Pallas kernels  72.2 us (99%)
  between operations  0.8 us (1%)
    pallas_call x1, Pallas kernels, device_step(): pl.pallas_call(functools.partial(main_kernel, n), out_shape=(pltpu.VMEM((...  69 us
    pallas_call x1, Pallas kernels, device_step(): pl.pallas_call(finish_kernel, out_shape=(row, row, row, jax.ShapeDtypeStr...  3.25 us

profile of v5, /device:TPU:81, one launch (start us, length us, event | category | flops | bytes accessed | tf_op | source)
XLA Modules:
  0.0 73.0 jit_solution(5341985490468387509)
XLA Ops:
  0.6 69.0 %decode_tail.1 = (bf16[64,128,512]{2,1,0:T(8,128)(2,1)S(1)}, f32[8,128]{1,0:T(8,128)S(1)}) custom-call(bf16[128,4096]{1,0:T(8,128)(2,1)} %h_hbm.1, bf16[4096,1792]{1,0:T(8,128)(2,1)} %wg_hbm.1, bf16[4096,1792]{1,0:T(8,128)(2,1)} %wu_hbm.1, bf16[1792,4096]{1,0:T(8,128)(2,1)} %wd_hbm.1, f32[1,4096]{1,0:T(1,128)} %bitcast.6, bf16[4096,4096]{1,0:T(8,128)(2,1)} %wv_hbm.1, ...), custom_call_target="tpu_custom_call" | custom-call | tf_op jit(solution)/shard_map/decode_tail/pallas_call | solution.py:449
  69.6 3.2 %write_log_probs.1 = (f32[1,128]{1,0:T(1,128)}, f32[1,128]{1,0:T(1,128)}, f32[1,128]{1,0:T(1,128)}, bf16[128,32768]{1,0:T(8,128)(2,1)}) custom-call(bf16[64,128,512]{2,1,0:T(8,128)(2,1)S(1)} %get-tuple-element.10.z_ref, f32[8,128]{1,0:T(8,128)S(1)} %get-tuple-element.11.fin_ref), custom_call_target="tpu_custom_call" | custom-call | tf_op jit(solution)/shard_map/write_log_probs/pallas_call | solution.py:486

commit v6 on v5

--- a/solution.py
+++ b/solution.py
@@ -18,7 +18,7 @@
 DOWN_SLOTS = 4
 SPLIT = (3, 5)
 GROUPS = len(SPLIT)
-RELAYED = 6
+RELAYED = (3, 6)
 TILE = 512
 FIRST, EARLY = 2, 6
 
@@ -32,11 +32,12 @@
         g = GROUPS
         self.part = self.take(chips)
         self.rs = self.take(g)
-        self.ynxt, self.yprv, self.yopp, self.ydie, self.fprv, self.fnxt, self.fopp = (self.take(g) for _ in range(7))
-        self.ytop, self.ybot, self.ftop, self.fbot = (self.take(g - 1) for _ in range(4))
-        self.znxt, self.zprv, self.zrel = (self.take(g * tiles) for _ in range(3))
-        self.zdie, self.zfar = self.take(tiles), self.take(tiles)
-        self.snxt, self.sprv, self.sopp, self.sdie, self.sfp, self.sfn, self.sfo = (self.take(1) for _ in range(7))
+        self.ynxt, self.yprv, self.yopp, self.ydie = (self.take(g) for _ in range(4))
+        self.ytop, self.ybot = (self.take(g - 1) for _ in range(2))
+        self.znear = self.take(g * tiles)
+        self.zrel = self.take(g * tiles // 2)
+        self.zdie, self.zfar = self.take(tiles // 2), self.take(tiles // 2)
+        self.stats, self.sdie = self.take(1), self.take(1)
 
     def take(self, k):
         first = self.count
@@ -121,7 +122,7 @@
 
     def down(k, dev):
         col = pl.ds(pl.multiple_of(dev * own_w, own_w), own_w)
-        return pltpu.make_async_copy(wd_hbm.at[:, col], dbuf.at[k % DOWN_SLOTS], dsem.at[k])
+        return pltpu.make_async_copy(wd_hbm.at[:, col], dbuf.at[k % DOWN_SLOTS], dsem.at[k % DOWN_SLOTS])
 
     plan = ((c_opp, 0, True), (c_nxt, 1, True), (c_prv, 2, True), (c_opp, 0, False),
             (c_nxt, 1, False), (c_prv, 2, False), (chip, 3, True), (chip, 3, False))
@@ -244,34 +245,28 @@
         return pl.ds(starts[g], top), pl.ds(starts[g] + top, sizes[g] - top)
 
     def forward_near(g):
-        for s, k, f in ((prv, ids.ynxt, ids.fprv), (nxt, ids.yprv, ids.fnxt)):
+        for s, k in ((prv, ids.ynxt), (nxt, ids.yprv)):
             arrived(ygat.at[s, g_rows(g)], k + g)
             if g > 0 and s is prv:
                 send(ygat.at[s, halves(g)[0]], ids.ytop + g - 1, nxt)
             elif g > 0:
                 send(ygat.at[s, halves(g)[1]], ids.ybot + g - 1, prv)
-            send(ygat.at[s, g_rows(g)], f + g, die)
+            send(ygat.at[s, g_rows(g)], ids.ydie + g, die)
 
     def forward_far(g):
         if g == 0:
             arrived(ygat.at[opp, g_rows(g)], ids.yopp + g)
-            send(ygat.at[opp, g_rows(g)], ids.fopp + g, die)
+            send(ygat.at[opp, g_rows(g)], ids.ydie + g, die)
             return
-        for rws, k, f in zip(halves(g), (ids.ytop, ids.ybot), (ids.ftop, ids.fbot)):
+        for rws, k in zip(halves(g), (ids.ytop, ids.ybot)):
             arrived(ygat.at[opp, rws], k + g - 1)
-            send(ygat.at[opp, rws], f + g - 1, die)
+            send(ygat.at[opp, rws], ids.ydie + g, die)
 
     def normalize(g):
         total_sq = squares(me, g) + squares(prv, g) + squares(nxt, g) + squares(opp, g)
-        for s, k in ((die, ids.ydie), (p_prv, ids.fprv), (p_nxt, ids.fnxt)):
-            arrived(ygat.at[s, g_rows(g)], k + g)
+        arrived(ygat.at[pl.ds(0, chips), g_rows(g)], ids.ydie + g)
+        for s in (die, p_prv, p_nxt, p_opp):
             total_sq += squares(s, g)
-        if g == 0:
-            arrived(ygat.at[p_opp, g_rows(g)], ids.fopp + g)
-        else:
-            for rws, k in zip(halves(g), (ids.ftop, ids.fbot)):
-                arrived(ygat.at[p_opp, rws], k + g - 1)
-        total_sq += squares(p_opp, g)
         inv_rms = lax.rsqrt(total_sq * (1.0 / dim) + NORM_EPS)
 
         @pl.loop(0, n)
@@ -286,8 +281,8 @@
     def own_sends(t, g):
         b = blk(me, t, g)
         at = g * tiles + t
-        return (remote(b, b, ids.znxt + at, nxt, SEND_Z), remote(b, b, ids.zprv + at, prv, SEND_Z),
-                remote(b, b, ids.zdie + t, die, SEND_Z))
+        return (remote(b, b, ids.znear + at, nxt, SEND_Z), remote(b, b, ids.znear + at, prv, SEND_Z),
+                remote(b, b, ids.zdie + t // 2, die, SEND_Z))
 
     def head(g, t0, t1):
         sl = g_slice(g)
@@ -316,14 +311,11 @@
     def near(g, t0, t1):
         for t in range(t0, t1):
             at = g * tiles + t
-            arrived(blk(prv, t, g), ids.znxt + at)
-            if t % 2 == 0:
-                send(blk(prv, t, g), ids.zrel + at, nxt, SEND_Z)
-            send(blk(prv, t, g), ids.zdie + t, die, SEND_Z)
-            arrived(blk(nxt, t, g), ids.zprv + at)
-            if t % 2 == 1:
-                send(blk(nxt, t, g), ids.zrel + at, prv, SEND_Z)
-            send(blk(nxt, t, g), ids.zdie + t, die, SEND_Z)
+            arrived(raw_ref.at[pl.ds(0, 2), g_rows(g)], ids.znear + at)
+            far = (blk(prv, t, g), nxt) if t % 2 == 0 else (blk(nxt, t, g), prv)
+            send(far[0], ids.zrel + at // 2, far[1], SEND_Z)
+            send(blk(prv, t, g), ids.zdie + t // 2, die, SEND_Z)
+            send(blk(nxt, t, g), ids.zdie + t // 2, die, SEND_Z)
 
     for g in range(GROUPS):
         sum_and_send(g)
@@ -338,9 +330,10 @@
         head(g, FIRST, EARLY)
         if more:
             forward_far(g + 1)
+            near(g, 0, RELAYED[0])
         head(g, EARLY, tiles)
         if more:
-            near(g, 0, RELAYED)
+            near(g, *RELAYED)
             normalize(g + 1)
 
     by_row = cols_ref[2].T
@@ -351,22 +344,17 @@
          jnp.sum(by_row[2 * tiles:3 * tiles] * scale, axis=0, keepdims=True),
          jnp.sum(by_row[3 * tiles:4 * tiles], axis=0, keepdims=True),
          jnp.zeros((st_ref.shape[1] - tiles - 3, rows), F32)], axis=0)
-    send(st_ref.at[me], ids.snxt, nxt, SEND_STATS)
-    send(st_ref.at[me], ids.sprv, prv, SEND_STATS)
-    send(st_ref.at[me], ids.sopp, opp, SEND_STATS)
+    for dev in (nxt, prv, opp):
+        send(st_ref.at[me], ids.stats, dev, SEND_STATS)
     send(st_ref.at[me], ids.sdie, die, SEND_STATS)
 
     for g in range(GROUPS):
-        near(g, RELAYED if g + 1 < GROUPS else 0, tiles)
-
-    arrived(st_ref.at[prv], ids.snxt)
-    send(st_ref.at[prv], ids.sfp, die, SEND_STATS)
-    arrived(st_ref.at[nxt], ids.sprv)
-    send(st_ref.at[nxt], ids.sfn, die, SEND_STATS)
-    arrived(st_ref.at[opp], ids.sopp)
-    send(st_ref.at[opp], ids.sfo, die, SEND_STATS)
-    for s, k in ((die, ids.sdie), (p_prv, ids.sfp), (p_nxt, ids.sfn), (p_opp, ids.sfo)):
-        arrived(st_ref.at[s], k)
+        near(g, RELAYED[1] if g + 1 < GROUPS else 0, tiles)
+
+    arrived(st_ref.at[pl.ds(0, 3)], ids.stats)
+    for dev in (prv, nxt, opp):
+        send(st_ref.at[dev], ids.sdie, die, SEND_STATS)
+    arrived(st_ref.at[pl.ds(0, chips)], ids.sdie)
 
     dev_top = jnp.max(st_ref[:, :tiles], axis=1)
     top = jnp.max(dev_top, axis=0, keepdims=True)
@@ -391,30 +379,35 @@
 
     def settle(items):
         for name, dev, t in items:
-            if name == "die" and ("die", t) not in seen:
-                arrived(raw_ref.at[pl.ds(0, 3)], ids.zdie + t)
-            if name == "far":
-                arrived(raw_ref.at[0], ids.zfar + t)
-            seen.add((name, t))
+            key = (name, t // 2)
+            if name == "die" and key not in seen:
+                arrived(raw_ref.at[pl.ds(0, 6)], ids.zdie + t // 2)
+            if name == "far" and key not in seen:
+                arrived(raw_ref.at[pl.ds(0, 2)], ids.zfar + t // 2)
+            seen.add(key)
         for _, dev, t in items:
             b = dev * tiles + t
             z_ref[b] = (raw_ref[b].astype(F32) + shift_ref[dev][:, t:t + 1]).astype(BF16)
 
-    steps = GROUPS * tiles
+    pairs = tiles // 2
+    steps = GROUPS * pairs
     taken = 0
     for g in range(GROUPS):
-        for t in range(tiles):
-            at = g * tiles + t
+        for p in range(pairs):
+            at = g * pairs + p
             upto = max(taken, (at * len(ready)) // (steps - 1))
             batch = ready[taken:upto]
             taken = upto
-            if g == GROUPS - 1 and t > 1:
-                batch += [("opp", opp, t - 2), ("far", p_opp, t - 2)]
-            settle(batch)
-            arrived(blk(opp, t, g), ids.zrel + at)
-            send(blk(opp, t, g), ids.zfar + t, die, SEND_Z)
-    settle([("opp", opp, tiles - 2), ("opp", opp, tiles - 1), ("far", p_opp, tiles - 2)])
-    settle([("far", p_opp, tiles - 1)])
+            for i in range(0, len(batch), 3):
+                settle(batch[i:i + 3])
+            if g == GROUPS - 1 and p > 1:
+                settle([(name, dev, 2 * p - 4 + i) for name, dev in (("opp", opp), ("far", p_opp)) for i in range(2)])
+            arrived(raw_ref.at[pl.ds(0, 2), g_rows(g)], ids.zrel + at)
+            for t in (2 * p, 2 * p + 1):
+                send(blk(opp, t, g), ids.zfar + p, die, SEND_Z)
+    settle([("opp", opp, tiles - 4 + i) for i in range(4)])
+    settle([("far", p_opp, tiles - 4 + i) for i in range(2)])
+    settle([("far", p_opp, tiles - 2 + i) for i in range(2)])
     for ref, kind in ((raw_ref.at[pl.ds(0, 2 * chips + 6)], SEND_Y), (raw_ref.at[pl.ds(0, 7 * tiles)], SEND_Z),
                       (st_ref.at[pl.ds(0, 7)], SEND_STATS)):
         remote(ref, ref, ids.part, die, kind).wait_send()
@@ -474,7 +467,7 @@
                 pltpu.SemaphoreType.DMA((n_ids,)),
                 pltpu.SemaphoreType.DMA((f_loc // SLAB + 1,)),
                 pltpu.SemaphoreType.DMA((tiles,)),
-                pltpu.SemaphoreType.DMA((n,)),
+                pltpu.SemaphoreType.DMA((DOWN_SLOTS,)),
                 pltpu.SemaphoreType.DMA((4,)),
             ],
             compiler_params=pltpu.CompilerParams(

time: 73.1 us -> 72.5 us (level)
  no operation moved by 1% of the time
where the time goes in v6:
time: 72.5 us; the launch traced here: 72.4 us
  Pallas kernels  71.6 us (99%)
  between operations  0.8 us (1%)
    pallas_call x1, Pallas kernels, device_step(): pl.pallas_call(functools.partial(main_kernel, n), out_shape=(pltpu.VMEM((...  68.4 us
    pallas_call x1, Pallas kernels, device_step(): pl.pallas_call(finish_kernel, out_shape=(row, row, row, jax.ShapeDtypeStr...  3.25 us

profile of v6, /device:TPU:81, one launch (start us, length us, event | category | flops | bytes accessed | tf_op | source)
XLA Modules:
  0.0 72.4 jit_solution(1330231007566316387)
XLA Ops:
  0.6 68.4 %decode_tail.1 = (bf16[64,128,512]{2,1,0:T(8,128)(2,1)S(1)}, f32[8,128]{1,0:T(8,128)S(1)}) custom-call(bf16[128,4096]{1,0:T(8,128)(2,1)} %h_hbm.1, bf16[4096,1792]{1,0:T(8,128)(2,1)} %wg_hbm.1, bf16[4096,1792]{1,0:T(8,128)(2,1)} %wu_hbm.1, bf16[1792,4096]{1,0:T(8,128)(2,1)} %wd_hbm.1, f32[1,4096]{1,0:T(1,128)} %bitcast.6, bf16[4096,4096]{1,0:T(8,128)(2,1)} %wv_hbm.1, ...), custom_call_target="tpu_custom_call" | custom-call | tf_op jit(solution)/shard_map/decode_tail/pallas_call | solution.py:442
  69.0 3.2 %write_log_probs.1 = (f32[1,128]{1,0:T(1,128)}, f32[1,128]{1,0:T(1,128)}, f32[1,128]{1,0:T(1,128)}, bf16[128,32768]{1,0:T(8,128)(2,1)}) custom-call(bf16[64,128,512]{2,1,0:T(8,128)(2,1)S(1)} %get-tuple-element.10.z_ref, f32[8,128]{1,0:T(8,128)S(1)} %get-tuple-element.11.fin_ref), custom_call_target="tpu_custom_call" | custom-call | tf_op jit(solution)/shard_map/write_log_probs/pallas_call | solution.py:479

commit v7 on v6

--- a/solution.py
+++ b/solution.py
@@ -16,7 +16,7 @@
 AHEAD = 3
 DOWN_AHEAD = 3
 DOWN_SLOTS = 4
-SPLIT = (3, 5)
+SPLIT = (4, 4)
 GROUPS = len(SPLIT)
 RELAYED = (3, 6)
 TILE = 512
@@ -203,12 +203,12 @@
         if q < 3:
             rsend[q] = total.astype(BF16)
             reduce_send(q, 0)
+            if q == 2:
+                for g in range(1, GROUPS):
+                    for r in range(3):
+                        reduce_send(r, g)
         else:
             own_ref[...] = total
-    for g in range(1, GROUPS):
-        for q in range(3):
-            reduce_send(q, g)
-
     for c in small[1:]:
         c.wait()
     row_ids = lax.broadcasted_iota(jnp.int32, (rows, rows), 0)

time: 72.5 us -> 72.1 us (level)
  no operation moved by 1% of the time
where the time goes in v7:
time: 72.1 us; the launch traced here: 72 us
  Pallas kernels  71.2 us (99%)
  between operations  0.8 us (1%)
    pallas_call x1, Pallas kernels, device_step(): pl.pallas_call(functools.partial(main_kernel, n), out_shape=(pltpu.VMEM((...  67.9 us
    pallas_call x1, Pallas kernels, device_step(): pl.pallas_call(finish_kernel, out_shape=(row, row, row, jax.ShapeDtypeStr...  3.25 us

profile of v7, /device:TPU:81, one launch (start us, length us, event | category | flops | bytes accessed | tf_op | source)
XLA Modules:
  0.0 72.0 jit_solution(113296697713753130)
XLA Ops:
  0.6 67.9 %decode_tail.1 = (bf16[64,128,512]{2,1,0:T(8,128)(2,1)S(1)}, f32[8,128]{1,0:T(8,128)S(1)}) custom-call(bf16[128,4096]{1,0:T(8,128)(2,1)} %h_hbm.1, bf16[4096,1792]{1,0:T(8,128)(2,1)} %wg_hbm.1, bf16[4096,1792]{1,0:T(8,128)(2,1)} %wu_hbm.1, bf16[1792,4096]{1,0:T(8,128)(2,1)} %wd_hbm.1, f32[1,4096]{1,0:T(1,128)} %bitcast.6, bf16[4096,4096]{1,0:T(8,128)(2,1)} %wv_hbm.1, ...), custom_call_target="tpu_custom_call" | custom-call | tf_op jit(solution)/shard_map/decode_tail/pallas_call | solution.py:442
  68.6 3.2 %write_log_probs.1 = (f32[1,128]{1,0:T(1,128)}, f32[1,128]{1,0:T(1,128)}, f32[1,128]{1,0:T(1,128)}, bf16[128,32768]{1,0:T(8,128)(2,1)}) custom-call(bf16[64,128,512]{2,1,0:T(8,128)(2,1)S(1)} %get-tuple-element.10.z_ref, f32[8,128]{1,0:T(8,128)S(1)} %get-tuple-element.11.fin_ref), custom_call_target="tpu_custom_call" | custom-call | tf_op jit(solution)/shard_map/write_log_probs/pallas_call | solution.py:479
